TPU v7x, 512 devices: a whole 4x8x8 slice. The times are simulated.
512 devices in a mesh: row: 32 (over z, x), col: 16 (over y, core).
Axes of the slice: x: 4, y: 8, z: 8, core: 2. Of those that a mesh axis runs over, the one named last changes fastest.
Arguments:
- matrix: float32 [16384, 16384], P('row', 'col'), may hold values from -300 to 300, as said below
Outputs:
- trailing: float32 [16384, 16384], P('row', 'col')
- reflectors: float32 [16384, 8], P('row')
Inputs may be any that keep to these rules, and one draw needn't show every extreme that they name: matrix is exactly symmetric.
All inputs are finite; a program needn't handle non-finite values.
Results may differ from a plain program's by a relative error of at most 0.00021.
Values sent between devices are 32-bit elements; how exact they have to be, the bound alone decides.
No kernel may reach another device: no remote copies, remote signals or barrier semaphores. Data moves between devices by JAX's collectives and lax.ppermute only.
A program may use at most 64 MiB of HBM per device.

v0:
```python
import jax
import jax.numpy as jnp
from jax import lax
from jax.sharding import PartitionSpec as P

N = 16384
COLS = 8


def picked(shard, axis, root):
    return lax.dynamic_index_in_dim(lax.all_gather(shard, axis), root, 0, keepdims=False)


def sent_to_all(shard, axis):
    size = lax.axis_size(axis)
    return lax.all_to_all(
        jnp.broadcast_to(shard[None], (size, *shard.shape)), axis, 0, 0, tiled=True
    )


def in_order(blocks, dim):
    dims = list(blocks.shape[1:])
    dims[dim] *= blocks.shape[0]
    return jnp.moveaxis(blocks, 0, dim).reshape(dims)


def gather_directly(shard, axis, dim):
    blocks = sent_to_all(shard, axis)
    return in_order(blocks, dim)


def of_everyone(shard, axis):
    return sent_to_all(shard, axis).sum(axis=0)


def precise_dot(operand, factor):
    return jnp.dot(
        operand, factor, precision=lax.Precision.HIGHEST, preferred_element_type=jnp.float32
    )


def local(matrix):
    rows_local = matrix.shape[0]
    cols_local = matrix.shape[1]
    row_index = lax.axis_index("row")
    col_index = lax.axis_index("col")
    panel = picked(matrix[:, :COLS], "col", 0)
    whole_panel = gather_directly(panel, "row", 0)
    all_ids = jnp.arange(whole_panel.shape[0], dtype=jnp.int32)
    reflect = jnp.zeros((N, COLS), jnp.float32)
    companion = jnp.zeros((N, COLS), jnp.float32)
    for column in range(COLS):
        reflect_rows = lax.dynamic_slice_in_dim(reflect, row_index * rows_local, rows_local, 0)
        companion_rows = lax.dynamic_slice_in_dim(companion, row_index * rows_local, rows_local, 0)
        current = (
            whole_panel[:, column]
            - precise_dot(reflect, companion[column])
            - precise_dot(companion, reflect[column])
        )
        below_whole = jnp.where(all_ids > column, current, 0.0)
        squared = jnp.sum(below_whole * below_whole)
        leading = jnp.sum(jnp.where(all_ids == column + 1, current, 0.0))
        length = jnp.sqrt(squared)
        vector = below_whole + jnp.where(all_ids == column + 1, length, 0.0)
        scaling = 1.0 / (length * (length + leading))
        vector_rows = lax.dynamic_slice_in_dim(vector, row_index * rows_local, rows_local, 0)
        vector_cols = lax.dynamic_slice_in_dim(vector, col_index * cols_local, cols_local, 0)
        weight_comp = precise_dot(companion.T, vector)
        weight_refl = precise_dot(reflect.T, vector)
        column_image = of_everyone(precise_dot(vector_rows, matrix), "row")
        reflect_cols = lax.dynamic_slice_in_dim(reflect, col_index * cols_local, cols_local, 0)
        companion_cols = lax.dynamic_slice_in_dim(companion, col_index * cols_local, cols_local, 0)
        pushed = scaling * (
            column_image
            - precise_dot(reflect_cols, weight_comp)
            - precise_dot(companion_cols, weight_refl)
        )
        inner_product = of_everyone(jnp.sum(pushed * vector_cols), "col")
        update_cols = pushed - 0.5 * scaling * inner_product * vector_cols
        update = gather_directly(update_cols, "col", 0)
        reflect = reflect.at[:, column].set(vector)
        companion = companion.at[:, column].set(update)
    reflect_rows = lax.dynamic_slice_in_dim(reflect, row_index * rows_local, rows_local, 0)
    companion_rows = lax.dynamic_slice_in_dim(companion, row_index * rows_local, rows_local, 0)
    reflect_cols = lax.dynamic_slice_in_dim(reflect, col_index * cols_local, cols_local, 0)
    companion_cols = lax.dynamic_slice_in_dim(companion, col_index * cols_local, cols_local, 0)
    trailing = (
        matrix
        - precise_dot(reflect_rows, companion_cols.T)
        - precise_dot(companion_rows, reflect_cols.T)
    )
    return (trailing, reflect_rows)


def solution(mesh):
    placed = (P("row", "col"),)
    return jax.shard_map(
        local,
        mesh=mesh,
        in_specs=placed,
        out_specs=(P("row", "col"), P("row", None)),
        check_vma=False,
    )
```

profile of v0, /device:TPU:1, one launch (start us, length us, event | category | flops | bytes accessed | tf_op | source)
XLA Modules:
  0.0 475.0 jit_solution(6673312461670348444)
XLA Ops:
  1.6 38.2 %all-gather = f32[8192,8]{1,0:T(8,128)S(1)} all-gather(f32[512,8]{1,0:T(8,128)S(1)} %slice.328), channel_id=2, replica_groups=mesh['row'=32,'col'=16] {'col'}, dimensions={0}, use_global_device_ids=true | all-gather | bytes 278528 | tf_op jit(solution)/shard_map/all_gather | solution.py:11
  40.8 8.5 %all-to-all-start = ((f32[32,512,8]{1,2,0:T(8,128)}), f32[32,512,8]{1,2,0:T(8,128)S(1)}, u32[]{:S(2)}, u32[]{:S(2)}) async-start(f32[32,512,8]{1,2,0:T(8,128)} %broadcast_in_dim.206), calls=%async_computation | async-start | bytes 1048576 | tf_op jit(solution)/shard_map/all_to_all | solution.py:16
  50.6 15.4 %all-to-all-done = f32[32,512,8]{1,2,0:T(8,128)S(1)} async-done(((f32[32,512,8]{1,2,0:T(8,128)}), f32[32,512,8]{1,2,0:T(8,128)S(1)}, u32[]{:S(2)}, u32[]{:S(2)}) %all-to-all-start) | async-done | bytes 524320 | tf_op jit(solution)/shard_map/all_to_all | solution.py:16
  71.5 5.0 %all-to-all-start.1 = ((f32[32,1,1024]{2,1,0:T(1,128)}), f32[32,1,1024]{2,1,0:T(1,128)S(1)}, u32[]{:S(2)}, u32[]{:S(2)}) async-start(f32[32,1,1024]{2,1,0:T(1,128)} %broadcast_in_dim.209), calls=%async_computation.1 | async-start | bytes 262144 | tf_op jit(solution)/shard_map/all_to_all | solution.py:16
  79.1 6.7 %all-to-all-done.1 = f32[32,1,1024]{2,1,0:T(1,128)S(1)} async-done(((f32[32,1,1024]{2,1,0:T(1,128)}), f32[32,1,1024]{2,1,0:T(1,128)S(1)}, u32[]{:S(2)}, u32[]{:S(2)}) %all-to-all-start.1) | async-done | bytes 131104 | tf_op jit(solution)/shard_map/all_to_all | solution.py:16
  88.5 8.2 %all-to-all-start.2 = ((f32[16,1,1]{2,1,0:T(1,128)}), f32[16,1,1]{2,1,0:T(1,128)S(1)}, u32[]{:S(2)}, u32[]{:S(2)}) async-start(f32[16,1,1]{2,1,0:T(1,128)} %broadcast_in_dim.210), calls=%async_computation.2 | async-start | bytes 16384 | tf_op jit(solution)/shard_map/all_to_all | solution.py:16
  96.7 7.0 %all-to-all-done.2 = f32[16,1,1]{2,1,0:T(1,128)S(1)} async-done(((f32[16,1,1]{2,1,0:T(1,128)}), f32[16,1,1]{2,1,0:T(1,128)S(1)}, u32[]{:S(2)}, u32[]{:S(2)}) %all-to-all-start.2) | async-done | bytes 96 | tf_op jit(solution)/shard_map/all_to_all | solution.py:16
  110.4 6.9 %all-to-all-done.3 = f32[16,1,1024]{2,1,0:T(1,128)S(1)} async-done(((f32[16,1,1024]{2,1,0:T(1,128)}), f32[16,1,1024]{2,1,0:T(1,128)S(1)}, u32[]{:S(2)}, u32[]{:S(2)}) %all-to-all-start.3) | async-done | bytes 65568 | tf_op jit(solution)/shard_map/all_to_all | solution.py:16
  130.6 8.9 %all-to-all-done.4 = f32[32,1,1024]{2,1,0:T(1,128)S(1)} async-done(((f32[32,1,1024]{2,1,0:T(1,128)}), f32[32,1,1024]{2,1,0:T(1,128)S(1)}, u32[]{:S(2)}, u32[]{:S(2)}) %all-to-all-start.4) | async-done | bytes 131104 | tf_op jit(solution)/shard_map/all_to_all | solution.py:16
  146.2 7.0 %all-to-all-done.5 = f32[16,1,1]{2,1,0:T(1,128)S(1)} async-done(((f32[16,1,1]{2,1,0:T(1,128)}), f32[16,1,1]{2,1,0:T(1,128)S(1)}, u32[]{:S(2)}, u32[]{:S(2)}) %all-to-all-start.5) | async-done | bytes 96 | tf_op jit(solution)/shard_map/all_to_all | solution.py:16
  155.2 5.2 %all-to-all-start.6 = ((f32[16,1,1024]{2,1,0:T(1,128)}), f32[16,1,1024]{2,1,0:T(1,128)}, u32[]{:S(2)}, u32[]{:S(2)}) async-start(f32[16,1,1024]{2,1,0:T(1,128)} %broadcast_in_dim.215), calls=%async_computation.6 | async-start | bytes 131072 | tf_op jit(solution)/shard_map/all_to_all | solution.py:16
  161.2 7.0 %all-to-all-done.6 = f32[16,1,1024]{2,1,0:T(1,128)} async-done(((f32[16,1,1024]{2,1,0:T(1,128)}), f32[16,1,1024]{2,1,0:T(1,128)}, u32[]{:S(2)}, u32[]{:S(2)}) %all-to-all-start.6) | async-done | bytes 65568 | tf_op jit(solution)/shard_map/all_to_all | solution.py:16
  182.1 8.9 %all-to-all-done.7 = f32[32,1,1024]{2,1,0:T(1,128)S(1)} async-done(((f32[32,1,1024]{2,1,0:T(1,128)}), f32[32,1,1024]{2,1,0:T(1,128)S(1)}, u32[]{:S(2)}, u32[]{:S(2)}) %all-to-all-start.7) | async-done | bytes 131104 | tf_op jit(solution)/shard_map/all_to_all | solution.py:16
  198.4 6.4 %all-to-all-done.8 = f32[16,1,1]{2,1,0:T(1,128)S(1)} async-done(((f32[16,1,1]{2,1,0:T(1,128)}), f32[16,1,1]{2,1,0:T(1,128)S(1)}, u32[]{:S(2)}, u32[]{:S(2)}) %all-to-all-start.8) | async-done | bytes 96 | tf_op jit(solution)/shard_map/all_to_all | solution.py:16
  212.0 6.5 %all-to-all-done.9 = f32[16,1,1024]{2,1,0:T(1,128)S(1)} async-done(((f32[16,1,1024]{2,1,0:T(1,128)}), f32[16,1,1024]{2,1,0:T(1,128)S(1)}, u32[]{:S(2)}, u32[]{:S(2)}) %all-to-all-start.9) | async-done | bytes 65568 | tf_op jit(solution)/shard_map/all_to_all | solution.py:16
  232.5 8.9 %all-to-all-done.10 = f32[32,1,1024]{2,1,0:T(1,128)S(1)} async-done(((f32[32,1,1024]{2,1,0:T(1,128)}), f32[32,1,1024]{2,1,0:T(1,128)S(1)}, u32[]{:S(2)}, u32[]{:S(2)}) %all-to-all-start.10) | async-done | bytes 131104 | tf_op jit(solution)/shard_map/all_to_all | solution.py:16
  248.8 6.3 %all-to-all-done.11 = f32[16,1,1]{2,1,0:T(1,128)S(1)} async-done(((f32[16,1,1]{2,1,0:T(1,128)}), f32[16,1,1]{2,1,0:T(1,128)S(1)}, u32[]{:S(2)}, u32[]{:S(2)}) %all-to-all-start.11) | async-done | bytes 96 | tf_op jit(solution)/shard_map/all_to_all | solution.py:16
  262.6 6.4 %all-to-all-done.12 = f32[16,1,1024]{2,1,0:T(1,128)S(1)} async-done(((f32[16,1,1024]{2,1,0:T(1,128)}), f32[16,1,1024]{2,1,0:T(1,128)S(1)}, u32[]{:S(2)}, u32[]{:S(2)}) %all-to-all-start.12) | async-done | bytes 65568 | tf_op jit(solution)/shard_map/all_to_all | solution.py:16
  283.0 8.9 %all-to-all-done.13 = f32[32,1,1024]{2,1,0:T(1,128)S(1)} async-done(((f32[32,1,1024]{2,1,0:T(1,128)}), f32[32,1,1024]{2,1,0:T(1,128)S(1)}, u32[]{:S(2)}, u32[]{:S(2)}) %all-to-all-start.13) | async-done | bytes 131104 | tf_op jit(solution)/shard_map/all_to_all | solution.py:16
  299.4 6.3 %all-to-all-done.14 = f32[16,1,1]{2,1,0:T(1,128)S(1)} async-done(((f32[16,1,1]{2,1,0:T(1,128)}), f32[16,1,1]{2,1,0:T(1,128)S(1)}, u32[]{:S(2)}, u32[]{:S(2)}) %all-to-all-start.14) | async-done | bytes 96 | tf_op jit(solution)/shard_map/all_to_all | solution.py:16
  313.1 6.4 %all-to-all-done.15 = f32[16,1,1024]{2,1,0:T(1,128)S(1)} async-done(((f32[16,1,1024]{2,1,0:T(1,128)}), f32[16,1,1024]{2,1,0:T(1,128)S(1)}, u32[]{:S(2)}, u32[]{:S(2)}) %all-to-all-start.15) | async-done | bytes 65568 | tf_op jit(solution)/shard_map/all_to_all | solution.py:16
  332.7 8.9 %all-to-all-done.16 = f32[32,1,1024]{2,1,0:T(1,128)S(1)} async-done(((f32[32,1,1024]{2,1,0:T(1,128)}), f32[32,1,1024]{2,1,0:T(1,128)S(1)}, u32[]{:S(2)}, u32[]{:S(2)}) %all-to-all-start.16) | async-done | bytes 131104 | tf_op jit(solution)/shard_map/all_to_all | solution.py:16
  343.5 5.2 %all-to-all-start.17 = ((f32[16,1,1]{2,1,0:T(1,128)}), f32[16,1,1]{2,1,0:T(1,128)S(1)}, u32[]{:S(2)}, u32[]{:S(2)}) async-start(f32[16,1,1]{2,1,0:T(1,128)} %broadcast_in_dim.230), calls=%async_computation.17 | async-start | bytes 16384 | tf_op jit(solution)/shard_map/all_to_all | solution.py:16
  349.4 6.2 %all-to-all-done.17 = f32[16,1,1]{2,1,0:T(1,128)S(1)} async-done(((f32[16,1,1]{2,1,0:T(1,128)}), f32[16,1,1]{2,1,0:T(1,128)S(1)}, u32[]{:S(2)}, u32[]{:S(2)}) %all-to-all-start.17) | async-done | bytes 96 | tf_op jit(solution)/shard_map/all_to_all | solution.py:16
  362.9 6.4 %all-to-all-done.18 = f32[16,1,1024]{2,1,0:T(1,128)S(1)} async-done(((f32[16,1,1024]{2,1,0:T(1,128)}), f32[16,1,1024]{2,1,0:T(1,128)S(1)}, u32[]{:S(2)}, u32[]{:S(2)}) %all-to-all-start.18) | async-done | bytes 65568 | tf_op jit(solution)/shard_map/all_to_all | solution.py:16
  382.5 8.9 %all-to-all-done.19 = f32[32,1,1024]{2,1,0:T(1,128)S(1)} async-done(((f32[32,1,1024]{2,1,0:T(1,128)}), f32[32,1,1024]{2,1,0:T(1,128)S(1)}, u32[]{:S(2)}, u32[]{:S(2)}) %all-to-all-start.19) | async-done | bytes 131104 | tf_op jit(solution)/shard_map/all_to_all | solution.py:16
  398.9 6.3 %all-to-all-done.20 = f32[16,1,1]{2,1,0:T(1,128)S(1)} async-done(((f32[16,1,1]{2,1,0:T(1,128)}), f32[16,1,1]{2,1,0:T(1,128)S(1)}, u32[]{:S(2)}, u32[]{:S(2)}) %all-to-all-start.20) | async-done | bytes 96 | tf_op jit(solution)/shard_map/all_to_all | solution.py:16
  412.6 6.4 %all-to-all-done.21 = f32[16,1,1024]{2,1,0:T(1,128)S(1)} async-done(((f32[16,1,1024]{2,1,0:T(1,128)}), f32[16,1,1024]{2,1,0:T(1,128)S(1)}, u32[]{:S(2)}, u32[]{:S(2)}) %all-to-all-start.21) | async-done | bytes 65568 | tf_op jit(solution)/shard_map/all_to_all | solution.py:16
  432.2 8.9 %all-to-all-done.22 = f32[32,1,1024]{2,1,0:T(1,128)S(1)} async-done(((f32[32,1,1024]{2,1,0:T(1,128)}), f32[32,1,1024]{2,1,0:T(1,128)S(1)}, u32[]{:S(2)}, u32[]{:S(2)}) %all-to-all-start.22) | async-done | bytes 131104 | tf_op jit(solution)/shard_map/all_to_all | solution.py:16
  443.0 5.1 %all-to-all-start.23 = ((f32[16,1,1]{2,1,0:T(1,128)}), f32[16,1,1]{2,1,0:T(1,128)S(1)}, u32[]{:S(2)}, u32[]{:S(2)}) async-start(f32[16,1,1]{2,1,0:T(1,128)} %broadcast_in_dim.238), calls=%async_computation.23 | async-start | bytes 16384 | tf_op jit(solution)/shard_map/all_to_all | solution.py:16
  448.1 7.0 %all-to-all-done.23 = f32[16,1,1]{2,1,0:T(1,128)S(1)} async-done(((f32[16,1,1]{2,1,0:T(1,128)}), f32[16,1,1]{2,1,0:T(1,128)S(1)}, u32[]{:S(2)}, u32[]{:S(2)}) %all-to-all-start.23) | async-done | bytes 96 | tf_op jit(solution)/shard_map/all_to_all | solution.py:16
  461.5 7.3 %all-to-all-done.24 = f32[16,1,1024]{2,1,0:T(1,128)S(1)} async-done(((f32[16,1,1024]{2,1,0:T(1,128)}), f32[16,1,1024]{2,1,0:T(1,128)S(1)}, u32[]{:S(2)}, u32[]{:S(2)}) %all-to-all-start.24) | async-done | bytes 65568 | tf_op jit(solution)/shard_map/all_to_all | solution.py:16
  (214 shorter events, 191.5 us)
Async XLA Ops:
  39.8 29.8 %copy-start = (f32[512,1024]{1,0:T(8,128)S(1)}, f32[512,1024]{1,0:T(8,128)}, u32[]{:S(2)}) copy-start(f32[512,1024]{1,0:T(8,128)} %param.33) | copy-start | bytes 6291460
  40.8 25.2 %all-to-all-start = ((f32[32,512,8]{1,2,0:T(8,128)}), f32[32,512,8]{1,2,0:T(8,128)S(1)}, u32[]{:S(2)}, u32[]{:S(2)}) async-start(f32[32,512,8]{1,2,0:T(8,128)} %broadcast_in_dim.206), calls=%async_computation | async-start | bytes 1048576 | tf_op jit(solution)/shard_map/all_to_all | solution.py:16
  71.5 14.4 %all-to-all-start.1 = ((f32[32,1,1024]{2,1,0:T(1,128)}), f32[32,1,1024]{2,1,0:T(1,128)S(1)}, u32[]{:S(2)}, u32[]{:S(2)}) async-start(f32[32,1,1024]{2,1,0:T(1,128)} %broadcast_in_dim.209), calls=%async_computation.1 | async-start | bytes 262144 | tf_op jit(solution)/shard_map/all_to_all | solution.py:16
  88.5 15.2 %all-to-all-start.2 = ((f32[16,1,1]{2,1,0:T(1,128)}), f32[16,1,1]{2,1,0:T(1,128)S(1)}, u32[]{:S(2)}, u32[]{:S(2)}) async-start(f32[16,1,1]{2,1,0:T(1,128)} %broadcast_in_dim.210), calls=%async_computation.2 | async-start | bytes 16384 | tf_op jit(solution)/shard_map/all_to_all | solution.py:16
  105.6 11.8 %all-to-all-start.3 = ((f32[16,1,1024]{2,1,0:T(1,128)}), f32[16,1,1024]{2,1,0:T(1,128)S(1)}, u32[]{:S(2)}, u32[]{:S(2)}) async-start(f32[16,1,1024]{2,1,0:T(1,128)} %broadcast_in_dim.211), calls=%async_computation.3 | async-start | bytes 131072 | tf_op jit(solution)/shard_map/all_to_all | solution.py:16
  125.7 13.8 %all-to-all-start.4 = ((f32[32,1,1024]{2,1,0:T(1,128)}), f32[32,1,1024]{2,1,0:T(1,128)S(1)}, u32[]{:S(2)}, u32[]{:S(2)}) async-start(f32[32,1,1024]{2,1,0:T(1,128)} %broadcast_in_dim.213), calls=%async_computation.4 | async-start | bytes 262144 | tf_op jit(solution)/shard_map/all_to_all | solution.py:16
  141.4 11.9 %all-to-all-start.5 = ((f32[16,1,1]{2,1,0:T(1,128)}), f32[16,1,1]{2,1,0:T(1,128)S(1)}, u32[]{:S(2)}, u32[]{:S(2)}) async-start(f32[16,1,1]{2,1,0:T(1,128)} %broadcast_in_dim.214), calls=%async_computation.5 | async-start | bytes 16384 | tf_op jit(solution)/shard_map/all_to_all | solution.py:16
  155.2 12.9 %all-to-all-start.6 = ((f32[16,1,1024]{2,1,0:T(1,128)}), f32[16,1,1024]{2,1,0:T(1,128)}, u32[]{:S(2)}, u32[]{:S(2)}) async-start(f32[16,1,1024]{2,1,0:T(1,128)} %broadcast_in_dim.215), calls=%async_computation.6 | async-start | bytes 131072 | tf_op jit(solution)/shard_map/all_to_all | solution.py:16
  177.2 13.8 %all-to-all-start.7 = ((f32[32,1,1024]{2,1,0:T(1,128)}), f32[32,1,1024]{2,1,0:T(1,128)S(1)}, u32[]{:S(2)}, u32[]{:S(2)}) async-start(f32[32,1,1024]{2,1,0:T(1,128)} %broadcast_in_dim.217), calls=%async_computation.7 | async-start | bytes 262144 | tf_op jit(solution)/shard_map/all_to_all | solution.py:16
  192.9 11.9 %all-to-all-start.8 = ((f32[16,1,1]{2,1,0:T(1,128)}), f32[16,1,1]{2,1,0:T(1,128)S(1)}, u32[]{:S(2)}, u32[]{:S(2)}) async-start(f32[16,1,1]{2,1,0:T(1,128)} %broadcast_in_dim.218), calls=%async_computation.8 | async-start | bytes 16384 | tf_op jit(solution)/shard_map/all_to_all | solution.py:16
  206.7 11.8 %all-to-all-start.9 = ((f32[16,1,1024]{2,1,0:T(1,128)}), f32[16,1,1024]{2,1,0:T(1,128)S(1)}, u32[]{:S(2)}, u32[]{:S(2)}) async-start(f32[16,1,1024]{2,1,0:T(1,128)} %broadcast_in_dim.219), calls=%async_computation.9 | async-start | bytes 131072 | tf_op jit(solution)/shard_map/all_to_all | solution.py:16
  227.6 13.8 %all-to-all-start.10 = ((f32[32,1,1024]{2,1,0:T(1,128)}), f32[32,1,1024]{2,1,0:T(1,128)S(1)}, u32[]{:S(2)}, u32[]{:S(2)}) async-start(f32[32,1,1024]{2,1,0:T(1,128)} %broadcast_in_dim.221), calls=%async_computation.10 | async-start | bytes 262144 | tf_op jit(solution)/shard_map/all_to_all | solution.py:16
  243.3 11.9 %all-to-all-start.11 = ((f32[16,1,1]{2,1,0:T(1,128)}), f32[16,1,1]{2,1,0:T(1,128)S(1)}, u32[]{:S(2)}, u32[]{:S(2)}) async-start(f32[16,1,1]{2,1,0:T(1,128)} %broadcast_in_dim.222), calls=%async_computation.11 | async-start | bytes 16384 | tf_op jit(solution)/shard_map/all_to_all | solution.py:16
  257.1 12.0 %all-to-all-start.12 = ((f32[16,1,1024]{2,1,0:T(1,128)}), f32[16,1,1024]{2,1,0:T(1,128)S(1)}, u32[]{:S(2)}, u32[]{:S(2)}) async-start(f32[16,1,1024]{2,1,0:T(1,128)} %broadcast_in_dim.223), calls=%async_computation.12 | async-start | bytes 131072 | tf_op jit(solution)/shard_map/all_to_all | solution.py:16
  278.1 13.8 %all-to-all-start.13 = ((f32[32,1,1024]{2,1,0:T(1,128)}), f32[32,1,1024]{2,1,0:T(1,128)S(1)}, u32[]{:S(2)}, u32[]{:S(2)}) async-start(f32[32,1,1024]{2,1,0:T(1,128)} %broadcast_in_dim.225), calls=%async_computation.13 | async-start | bytes 262144 | tf_op jit(solution)/shard_map/all_to_all | solution.py:16
  293.9 11.9 %all-to-all-start.14 = ((f32[16,1,1]{2,1,0:T(1,128)}), f32[16,1,1]{2,1,0:T(1,128)S(1)}, u32[]{:S(2)}, u32[]{:S(2)}) async-start(f32[16,1,1]{2,1,0:T(1,128)} %broadcast_in_dim.226), calls=%async_computation.14 | async-start | bytes 16384 | tf_op jit(solution)/shard_map/all_to_all | solution.py:16
  307.7 11.8 %all-to-all-start.15 = ((f32[16,1,1024]{2,1,0:T(1,128)}), f32[16,1,1024]{2,1,0:T(1,128)S(1)}, u32[]{:S(2)}, u32[]{:S(2)}) async-start(f32[16,1,1024]{2,1,0:T(1,128)} %broadcast_in_dim.227), calls=%async_computation.15 | async-start | bytes 131072 | tf_op jit(solution)/shard_map/all_to_all | solution.py:16
  327.8 13.8 %all-to-all-start.16 = ((f32[32,1,1024]{2,1,0:T(1,128)}), f32[32,1,1024]{2,1,0:T(1,128)S(1)}, u32[]{:S(2)}, u32[]{:S(2)}) async-start(f32[32,1,1024]{2,1,0:T(1,128)} %broadcast_in_dim.229), calls=%async_computation.16 | async-start | bytes 262144 | tf_op jit(solution)/shard_map/all_to_all | solution.py:16
  343.5 12.1 %all-to-all-start.17 = ((f32[16,1,1]{2,1,0:T(1,128)}), f32[16,1,1]{2,1,0:T(1,128)S(1)}, u32[]{:S(2)}, u32[]{:S(2)}) async-start(f32[16,1,1]{2,1,0:T(1,128)} %broadcast_in_dim.230), calls=%async_computation.17 | async-start | bytes 16384 | tf_op jit(solution)/shard_map/all_to_all | solution.py:16
  357.6 11.7 %all-to-all-start.18 = ((f32[16,1,1024]{2,1,0:T(1,128)}), f32[16,1,1024]{2,1,0:T(1,128)S(1)}, u32[]{:S(2)}, u32[]{:S(2)}) async-start(f32[16,1,1024]{2,1,0:T(1,128)} %broadcast_in_dim.231), calls=%async_computation.18 | async-start | bytes 131072 | tf_op jit(solution)/shard_map/all_to_all | solution.py:16
  377.6 13.8 %all-to-all-start.19 = ((f32[32,1,1024]{2,1,0:T(1,128)}), f32[32,1,1024]{2,1,0:T(1,128)S(1)}, u32[]{:S(2)}, u32[]{:S(2)}) async-start(f32[32,1,1024]{2,1,0:T(1,128)} %broadcast_in_dim.233), calls=%async_computation.19 | async-start | bytes 262144 | tf_op jit(solution)/shard_map/all_to_all | solution.py:16
  393.3 11.9 %all-to-all-start.20 = ((f32[16,1,1]{2,1,0:T(1,128)}), f32[16,1,1]{2,1,0:T(1,128)S(1)}, u32[]{:S(2)}, u32[]{:S(2)}) async-start(f32[16,1,1]{2,1,0:T(1,128)} %broadcast_in_dim.234), calls=%async_computation.20 | async-start | bytes 16384 | tf_op jit(solution)/shard_map/all_to_all | solution.py:16
  407.2 11.8 %all-to-all-start.21 = ((f32[16,1,1024]{2,1,0:T(1,128)}), f32[16,1,1024]{2,1,0:T(1,128)S(1)}, u32[]{:S(2)}, u32[]{:S(2)}) async-start(f32[16,1,1024]{2,1,0:T(1,128)} %broadcast_in_dim.235), calls=%async_computation.21 | async-start | bytes 131072 | tf_op jit(solution)/shard_map/all_to_all | solution.py:16
  427.3 13.8 %all-to-all-start.22 = ((f32[32,1,1024]{2,1,0:T(1,128)}), f32[32,1,1024]{2,1,0:T(1,128)S(1)}, u32[]{:S(2)}, u32[]{:S(2)}) async-start(f32[32,1,1024]{2,1,0:T(1,128)} %broadcast_in_dim.237), calls=%async_computation.22 | async-start | bytes 262144 | tf_op jit(solution)/shard_map/all_to_all | solution.py:16
  443.0 12.1 %all-to-all-start.23 = ((f32[16,1,1]{2,1,0:T(1,128)}), f32[16,1,1]{2,1,0:T(1,128)S(1)}, u32[]{:S(2)}, u32[]{:S(2)}) async-start(f32[16,1,1]{2,1,0:T(1,128)} %broadcast_in_dim.238), calls=%async_computation.23 | async-start | bytes 16384 | tf_op jit(solution)/shard_map/all_to_all | solution.py:16
  457.0 11.8 %all-to-all-start.24 = ((f32[16,1,1024]{2,1,0:T(1,128)}), f32[16,1,1024]{2,1,0:T(1,128)S(1)}, u32[]{:S(2)}, u32[]{:S(2)}) async-start(f32[16,1,1024]{2,1,0:T(1,128)} %broadcast_in_dim.239), calls=%async_computation.24 | async-start | bytes 131072 | tf_op jit(solution)/shard_map/all_to_all | solution.py:16
  461.5 13.0 %copy-start.1 = (f32[512,8]{0,1:T(8,128)}, f32[512,8]{0,1:T(8,128)S(1)}, u32[]{:S(2)}) copy-start(f32[512,8]{0,1:T(8,128)S(1)} %constant_dynamic-slice_fusion) | copy-start | bytes 49156
where the time goes:
time: 484 us; the launch traced here: 475 us
  waiting for transfers between devices  190 us (39%)
  starting transfers between devices  116 us (24%)
  matrix products  43.4 us (9%)
  blocking collectives  38.2 us (8%)
  local copies, waits for them, and re-layouts  35.5 us (7%)
  other arithmetic  33.4 us (7%)
  between operations  18.1 us (4%)
    all_to_all x25, waiting for transfers between devices, sent_to_all(): lax.all_to_all(jnp.broadcast_to(shard[None], (size, *shard.shape)), axis,...  190 us
    all_to_all x25, starting transfers between devices, sent_to_all(): lax.all_to_all(jnp.broadcast_to(shard[None], (size, *shard.shape)), axis,...  116 us
    dot_general x53, matrix products, precise_dot(): jnp.dot(operand, factor, precision=lax.Precision.HIGHEST, preferred_eleme...  43.4 us
    all_gather x1, blocking collectives, picked(): lax.all_gather(shard, axis)  38.2 us
    broadcast_in_dim x25, local copies, waits for them, and re-layouts, sent_to_all(): jnp.broadcast_to(shard[None], (size, *shard.shape))  22 us
    another operation x21, other arithmetic  15.4 us
  transfers between devices with their start and end apart: 25, of which 25 were waited for; matrix products, arithmetic and copies ran while one was open for 4% of the time, Pallas kernels for 0%

commit v1 on v0

v1 whole, which is shorter than its diff:
```python
import functools

import jax
import jax.numpy as jnp
from jax import lax
from jax.experimental import pallas as pl
from jax.experimental.pallas import tpu as pltpu
from jax.sharding import PartitionSpec as P


N = 16384
COLS = 8
LANES = 128
F32 = jnp.float32
VMEM = pltpu.VMEM
LIMIT = 16 << 20


def total(x):
    return jnp.sum(jnp.sum(x, axis=0, keepdims=True), axis=1, keepdims=True)


def iota(shape, dim):
    return lax.broadcasted_iota(jnp.int32, shape, dim)


def without_first(x, owner):
    hit = (iota(x.shape, 0) == 0) & (iota(x.shape, 1) == 0)
    if owner is not None:
        hit = hit & (owner == 0)
    return jnp.where(hit, 0.0, x)


def times_rows(a_ref, x):
    upright = jnp.concatenate([x, jnp.zeros_like(x)], axis=0).T
    out = []
    for t in range(8):
        acc = jnp.zeros((8, LANES), F32)
        for q in range(4):
            block = a_ref[q * LANES : (q + 1) * LANES, t * LANES : (t + 1) * LANES]
            acc = acc + jnp.sum((block * upright[:, q : q + 1]).reshape(16, 8, LANES), axis=0)
        out.append(jnp.sum(acc, axis=0, keepdims=True))
    return jnp.concatenate(out, axis=0)


def times_cols(a_ref, x):
    out = []
    for q in range(4):
        acc = jnp.zeros((LANES, LANES), F32)
        for t in range(8):
            block = a_ref[q * LANES : (q + 1) * LANES, t * LANES : (t + 1) * LANES]
            acc = acc + block * x[t : t + 1, :]
        out.append(jnp.sum(acc.T, axis=0, keepdims=True))
    return jnp.concatenate(out, axis=0)


def send_all(send_ref, first, parts):
    for member in range(send_ref.shape[0]):
        for k, part in enumerate(parts):
            send_ref[member, first + k] = part


def halves(x):
    return [x[:4], x[4:]]


def along_cols(recv_ref):
    s = jnp.sum(recv_ref[:, 0:2], axis=0)
    return jnp.concatenate([s[0], s[1]], axis=0)


def along_rows(recv_ref):
    return jnp.sum(recv_ref[:, 0], axis=0)


def whole_from_rows(recv_ref, group):
    return jnp.concatenate([recv_ref[r, group] for r in range(recv_ref.shape[0])], axis=0)


def whole_from_cols(recv_ref, group):
    return jnp.concatenate(
        [recv_ref[c, group + k] for c in range(recv_ref.shape[0]) for k in range(2)], axis=0
    )


def start_kernel(a_ref, held_ref, send_ref):
    held_ref[...] = a_ref[...]
    left = [a_ref[q * LANES : (q + 1) * LANES, 0:LANES].T for q in range(4)]
    column = jnp.concatenate([x[0:1] for x in left], axis=0)
    corner = a_ref[0:16, 0:LANES]
    packed = jnp.zeros((1, LANES), F32)
    for j in range(COLS):
        lanes = iota((1, LANES), 1)
        entry = jnp.where(lanes < 16, corner[j + 1 : j + 2], 0.0)
        packed = packed + (pltpu.roll(entry, 16 * j, 1) if j else entry)
    blank = jnp.zeros((1, LANES), F32)
    for member in range(16):
        j, half = member // 2, member % 2
        rows = [left[2 * half + k][j + 1 : j + 2] for k in range(2)]
        send_ref[member, 0] = column
        send_ref[member, 1] = jnp.concatenate([*rows, packed, blank], axis=0)


def first_kernel(ids_ref, a_ref, recv_ref, send_ref, piece_ref):
    column = recv_ref[0, 0]
    piece_ref[...] = recv_ref[0, 1]
    packed = recv_ref[0, 1][2:3]
    send_all(send_ref, 0, halves(times_rows(a_ref, without_first(column, ids_ref[0]))))
    send_all(send_ref, 2, [column])
    blank = jnp.zeros((1, LANES), F32)
    for member in range(32):
        j, quarter = member // 4, member % 4
        rows = [
            a_ref[j + 1 : j + 2, (2 * quarter + k) * LANES : (2 * quarter + k + 1) * LANES]
            for k in range(2)
        ]
        send_ref[member, 3] = jnp.concatenate([*rows, packed, blank], axis=0)


def coefficient(scal, k):
    return scal[k : k + 1, 0:1]


def settle(step, y_whole, scal, qs, aqs):
    if step == 2:
        aq = None
        u = without_first(y_whole, None)
    else:
        aq = y_whole
        for i in range(1, step - 2):
            aq = aq - coefficient(scal, i) * aqs[i]
        aq = aq * coefficient(scal, 8)
        u = aq
        if step > 3:
            u = u - coefficient(scal, 0) * qs[step - 3]
        u = without_first(u, None)
    known = range(1, step - 1)
    rows = [jnp.sum(u * qs[i], axis=0, keepdims=True) for i in known]
    w = u
    cs = {}
    if rows:
        rows = rows + [jnp.zeros((1, LANES), F32)] * (8 - len(rows))
        sums = jnp.sum(jnp.concatenate(rows, axis=0), axis=1, keepdims=True)
        for i in known:
            cs[i] = sums[i - 1 : i, 0:1]
            w = w - cs[i] * qs[i]
    length = jnp.sqrt(total(w * w))
    inverse = 1.0 / length
    zero = jnp.zeros((1, LANES), F32)
    out = [zero + length] + [zero + cs[i] if i in cs else zero for i in range(1, 8)]
    out = out + [zero + inverse] + [zero] * 7
    return aq, w * inverse, length, inverse, cs, jnp.concatenate(out, axis=0)


def step_kernel(step, *refs):
    refs = list(refs)
    ids_ref, a_ref, recv_ref = refs[:3]
    del refs[:3]
    piece_ref = refs.pop(0) if step in (2, 3) else None
    scal = refs.pop(0)[...] if step > 2 else None
    q_refs = {i: refs.pop(0) for i in range(1, step - 1)}
    aq_refs = {i: refs.pop(0) for i in range(1, step - 2)}
    send_ref = refs.pop(0)
    q_ref = refs.pop(0)
    aq_ref = refs.pop(0) if step > 2 else None
    scal_ref = refs.pop(0)
    edge_ref = refs.pop(0) if step in (3, 4) else None
    new_piece_ref = refs.pop(0) if step == 2 else None

    even = step % 2 == 0
    if even:
        y_here = along_cols(recv_ref)
        y_whole = whole_from_rows(recv_ref, 2)
        chunk, rows = ids_ref[1], 8
    else:
        y_here = along_rows(recv_ref)
        y_whole = whole_from_cols(recv_ref, 1)
        chunk, rows = ids_ref[0], 4
    aq, q, length, inverse, cs, scal_out = settle(
        step,
        y_whole,
        scal,
        {i: r[...] for i, r in q_refs.items()},
        {i: r[...] for i, r in aq_refs.items()},
    )
    q_ref[...] = q
    scal_ref[...] = scal_out
    if aq_ref is not None:
        aq_ref[...] = aq
    at = pl.ds(chunk * rows, rows)
    here = y_here
    for i in cs:
        source = aq_ref if i == step - 2 else aq_refs[i]
        here = here - cs[i] * source[at, :]
    here = here * inverse
    if step > 2:
        here = here - length * q_refs[step - 2][at, :]
    here = without_first(here, chunk)
    if even:
        send_all(send_ref, 0, [times_cols(a_ref, here)])
        send_all(send_ref, 1, halves(y_here))
    else:
        send_all(send_ref, 0, halves(times_rows(a_ref, here)))
        send_all(send_ref, 2, [y_here])
    if step in (2, 3):
        send_all(send_ref, 3, [piece_ref[...]])
    if step == 2:
        new_piece_ref[...] = recv_ref[0, 3]
    if step == 3:
        edge_ref[...] = jnp.concatenate([recv_ref[c, 3][0:2] for c in range(16)], axis=0)
    if step == 4:
        edge_ref[...] = jnp.concatenate([recv_ref[r, 3][0:2] for r in range(32)], axis=0)


def last_send_kernel(recv_ref, send_ref):
    send_all(send_ref, 0, [along_rows(recv_ref)])


def sign(k):
    return -1.0 if k % 2 else 1.0


def product(x, y):
    return lax.dot_general(
        x,
        y,
        (((0,), (0,)), ((), ())),
        precision=lax.Precision.HIGHEST,
        preferred_element_type=F32,
    )


def rows_at(refs, row):
    return jnp.concatenate([sign(k) * refs[k][pl.ds(row, 1), :] for k in range(1, 9)], axis=0)


def d_tile(q_refs, row):
    lanes, ks = iota((8, LANES), 1), iota((8, LANES), 0)
    unit = jnp.where((lanes == ks + 1) & (row == 0), 1.0, 0.0)
    return unit - rows_at(q_refs, row)


def panel_kernel(*refs):
    refs = list(refs)
    ids_ref, recv_ref = refs[:2]
    scal_refs = {i: refs[1 + i] for i in range(1, 8)}
    q_refs = {i: refs[8 + i] for i in range(1, 8)}
    aq_refs = {i: refs[15 + i] for i in range(1, 7)}
    q_out, aq_out, scal_out, factor_ref, reflect_ref = refs[22:27]
    y_whole = whole_from_cols(recv_ref, 1)
    aq, q, _, _, _, scal = settle(
        9,
        y_whole,
        scal_refs[7][...],
        {i: r[...] for i, r in q_refs.items()},
        {i: r[...] for i, r in aq_refs.items()},
    )
    q_out[...] = q
    aq_out[...] = aq
    scal_out[...] = scal
    q_refs[8] = q_out
    lanes, ks = iota((8, LANES), 1), iota((8, LANES), 0)
    top = d_tile(q_refs, 0)
    work = jnp.where(lanes < 8, pltpu.roll(top, LANES - 1, 1), 0.0)
    work = work + jnp.where(lanes == ks + 8, 1.0, 0.0)
    to_reflect = jnp.zeros((8, LANES), F32)
    for k in range(8):
        row = work[k : k + 1]
        beta = (scal if k == 7 else scal_refs[k + 1])[0:1, :]
        to_reflect = jnp.where(ks == k, row * beta, to_reflect)
        row = row / row[:, k : k + 1]
        column = jnp.where(ks == k, 0.0, work)[:, k : k + 1]
        work = jnp.where(ks == k, row, work - column * row)
    factor_ref[...] = jnp.where(lanes < 8, pltpu.roll(work, LANES - 8, 1), 0.0)
    to_reflect = jnp.where(lanes < 8, pltpu.roll(to_reflect, LANES - 8, 1), 0.0)
    for t in range(4):
        row = 4 * ids_ref[0] + t
        d = d_tile(q_refs, row)
        out = jnp.zeros((8, LANES), F32)
        for k in range(8):
            out = out + to_reflect[:, k : k + 1] * d[k : k + 1, :]
        out = jnp.where((row == 0) & (lanes <= ks), 0.0, out)
        reflect_ref[:, t * LANES : (t + 1) * LANES] = out


def trailing_kernel(*refs):
    refs = list(refs)
    ids_ref, a_ref, recv_ref, packed_ref, edge_r_ref, edge_c_ref, factor_ref = refs[:7]
    scal_refs = {i: refs[6 + i] for i in range(1, 9)}
    q_refs = {i: refs[14 + i] for i in range(1, 9)}
    aq_refs = {i: refs[22 + i] for i in range(1, 8)}
    out_ref, last_ref, left_ref, right_ref = refs[30:34]
    scal = scal_refs[8][...]
    aq = whole_from_rows(recv_ref, 0)
    for i in range(1, 8):
        aq = aq - coefficient(scal, i) * aq_refs[i][...]
    aq = aq * coefficient(scal, 8)
    last_ref[...] = aq
    aq_refs[8] = last_ref
    lanes, ks = iota((8, LANES), 1), iota((8, LANES), 0)
    factor = factor_ref[...]
    inner = jnp.zeros((8, LANES), F32)
    packed = packed_ref[2:3]
    for j in range(8):
        entry = pltpu.roll(packed, LANES - 16 * j, 1) if j else packed
        inner = jnp.where(ks == j, entry, inner)
    inner = jnp.where((lanes >= 1) & (lanes <= 8), inner, 0.0)
    cross = rows_at(aq_refs, 0)
    cross = jnp.where((lanes >= 1) & (lanes <= 8), cross, 0.0)
    inner = pltpu.roll(inner - cross, LANES - 1, 1)
    cross = pltpu.roll(cross, LANES - 1, 1)
    square = jnp.concatenate([cross, jnp.zeros((LANES - 8, LANES), F32)], axis=0)
    inner = inner - square.T[0:8]
    for k in range(1, 9):
        if k < 8:
            alpha = scal_refs[k + 1][k : k + 1, :]
            beta = scal_refs[k + 1][0:1, :]
            near = ((ks == k - 1) & (lanes == k)) | ((ks == k) & (lanes == k - 1))
            inner = inner - jnp.where(near, beta, 0.0)
        else:
            alpha = total(q_refs[8][...] * aq)
        inner = inner + jnp.where((ks == k - 1) & (lanes == k - 1), alpha, 0.0)
    factor = factor[:, 0:8]
    inner = inner[:, 0:8]
    core = product(factor, product(inner, factor))

    def tiles(base, count, edge_ref):
        ds, ys = [], []
        for t in range(count):
            row = base + t
            d = d_tile(q_refs, row)
            edge = jnp.concatenate(
                [edge_ref[count * j + t : count * j + t + 1, :] for j in range(8)], axis=0
            )
            ad = edge - rows_at(aq_refs, row)
            ds.append(d)
            ys.append(product(factor, ad) - 0.5 * product(core, d))
        return ds, ys

    ds, ys = tiles(4 * ids_ref[0], 4, edge_r_ref)
    for t in range(4):
        left_ref[0:8, t * LANES : (t + 1) * LANES] = ds[t]
        left_ref[8:16, t * LANES : (t + 1) * LANES] = ys[t]
    ds, ys = tiles(8 * ids_ref[1], 8, edge_c_ref)
    for t in range(8):
        right_ref[0:8, t * LANES : (t + 1) * LANES] = ys[t]
        right_ref[8:16, t * LANES : (t + 1) * LANES] = ds[t]
    for q in range(4):
        at = slice(q * LANES, (q + 1) * LANES)
        out_ref[at, :] = a_ref[at, :] - product(left_ref[:, at], right_ref[...])


def call(kernel, outs, *args, scratch=(), pinned=True, flops=1000):
    def spec(x):
        return pl.BlockSpec(memory_space=pltpu.SMEM if x.dtype == jnp.int32 else VMEM)

    return pl.pallas_call(
        kernel,
        out_shape=[VMEM(s, F32) if pinned else jax.ShapeDtypeStruct(s, F32) for s in outs],
        in_specs=[spec(x) for x in args],
        out_specs=[pl.BlockSpec(memory_space=VMEM)] * len(outs),
        scratch_shapes=[VMEM(s, F32) for s in scratch],
        compiler_params=pltpu.CompilerParams(vmem_limit_bytes=LIMIT),
        cost_estimate=pl.CostEstimate(flops=flops, bytes_accessed=1000, transcendentals=0),
    )(*args)


def exchange(x, axis):
    return lax.all_to_all(x, axis, 0, 0, tiled=True)


def local(matrix):
    ids = jnp.stack([lax.axis_index("row"), lax.axis_index("col")]).astype(jnp.int32)
    whole = (N // LANES, LANES)
    held, send = call(start_kernel, [matrix.shape, (16, 2, 4, LANES)], matrix)
    recv = exchange(send, "col")
    send, piece = call(first_kernel, [(32, 4, 4, LANES), (4, LANES)], ids, held, recv)
    recv = exchange(send, "row")
    qs, aqs, scals = {}, {}, {}
    for step in range(2, 9):
        args = [ids, held, recv]
        if step in (2, 3):
            args.append(piece)
        if step > 2:
            args.append(scals[step - 2])
        args += [qs[i] for i in range(1, step - 1)] + [aqs[i] for i in range(1, step - 2)]
        groups = 4 if step in (2, 3) else 3
        outs = [(16 if step % 2 == 0 else 32, groups, 4, LANES), whole]
        if step > 2:
            outs.append(whole)
        outs.append((16, LANES))
        if step in (3, 4):
            outs.append((32 if step == 3 else 64, LANES))
        if step == 2:
            outs.append((4, LANES))
        result = list(call(functools.partial(step_kernel, step), outs, *args))
        send = result.pop(0)
        qs[step - 1] = result.pop(0)
        if step > 2:
            aqs[step - 2] = result.pop(0)
        scals[step - 1] = result.pop(0)
        if step == 3:
            edge_r = result.pop(0)
        if step == 4:
            edge_c = result.pop(0)
        if step == 2:
            piece = packed = result.pop(0)
        recv = exchange(send, "col" if step % 2 == 0 else "row")
    (send,) = call(last_send_kernel, [(32, 1, 4, LANES)], recv)
    last = exchange(send, "row")
    qs[8], aqs[7], scals[8], factor, reflect = call(
        panel_kernel,
        [whole, whole, (16, LANES), (8, LANES), (8, matrix.shape[0])],
        ids,
        recv,
        *[scals[i] for i in range(1, 8)],
        *[qs[i] for i in range(1, 8)],
        *[aqs[i] for i in range(1, 7)],
        flops=40000000,
    )
    (trailing,) = call(
        trailing_kernel,
        [matrix.shape],
        ids,
        held,
        last,
        packed,
        edge_r,
        edge_c,
        factor,
        *[scals[i] for i in range(1, 9)],
        *[qs[i] for i in range(1, 9)],
        *[aqs[i] for i in range(1, 8)],
        scratch=[whole, (16, 512), (16, 1024)],
        pinned=False,
    )
    return trailing, reflect.T


def solution(mesh):
    placed = (P("row", "col"),)
    return jax.shard_map(
        local,
        mesh=mesh,
        in_specs=placed,
        out_specs=(P("row", "col"), P("row", None)),
        check_vma=False,
    )
```

time: 484 us -> 167 us (0.35); the launches traced: 475 us -> 166 us
  waiting for transfers between devices: 190 us -> 14.7 us
  starting transfers between devices: 116 us -> 14 us
  blocking collectives: 38.2 us -> 118 us
  matrix products: 43.4 us -> 0 us
  other arithmetic: 33.4 us -> 0.07 us
  local copies, waits for them, and re-layouts: 35.5 us -> 2.19 us
  between operations: 18.1 us -> 0.72 us
  Pallas kernels: 0 us -> 15.8 us
    all_to_all x25 -> x2, waiting for transfers between devices: 190 us -> 14.7 us  [exchange(): return lax.all_to_all(x, axis, 0, 0, tiled=True)]
    all_to_all x0 -> x8, blocking collectives: none -> 118 us  [exchange(): return lax.all_to_all(x, axis, 0, 0, tiled=True)]
    all_to_all x25 -> x2, starting transfers between devices: 116 us -> 14 us  [exchange(): return lax.all_to_all(x, axis, 0, 0, tiled=True)]
    dot_general x53 -> x0, matrix products: 43.4 us -> none  [precise_dot(): jnp.dot(operand, factor, precision=lax.Precision.HIGHEST, preferred_eleme...]
    all_gather x1 -> x0, blocking collectives: 38.2 us -> none  [picked(): lax.all_gather(shard, axis)]
    broadcast_in_dim x25 -> x0, local copies, waits for them, and re-layouts: 22 us -> none  [sent_to_all(): jnp.broadcast_to(shard[None], (size, *shard.shape))]
    reduce_sum x32 -> x0, other arithmetic: 17.2 us -> none  [the longest x8 6.66 us: local(): leading = jnp.sum(jnp.where(all_ids == column + 1, current, 0.0))]
    pallas_call x0 -> x12, Pallas kernels: none -> 15.8 us  [call(): pl.pallas_call(kernel, out_shape=[VMEM(s, F32) if pinned else jax.ShapeDt...]
  transfers between devices with their start and end apart: 25 -> 2, of which waited for: 25 -> 2; matrix products, arithmetic and copies ran while one was open for 4% -> 0% of each run, Pallas kernels for 0% -> 1%
where the time goes in v1:
time: 167 us; the launch traced here: 166 us
  blocking collectives  118 us (71%)
  Pallas kernels  15.8 us (9%)
  waiting for transfers between devices  14.7 us (9%)
  starting transfers between devices  14 us (8%)
  local copies, waits for them, and re-layouts  2.19 us (1%)
    all_to_all x8, blocking collectives, exchange(): return lax.all_to_all(x, axis, 0, 0, tiled=True)  118 us
    pallas_call x12, Pallas kernels, call(): pl.pallas_call(kernel, out_shape=[VMEM(s, F32) if pinned else jax.ShapeDt...  15.8 us
    all_to_all x2, waiting for transfers between devices, exchange(): return lax.all_to_all(x, axis, 0, 0, tiled=True)  14.7 us
    all_to_all x2, starting transfers between devices, exchange(): return lax.all_to_all(x, axis, 0, 0, tiled=True)  14 us
  transfers between devices with their start and end apart: 2, of which 2 were waited for; matrix products, arithmetic and copies ran while one was open for 0% of the time, Pallas kernels for 1%

profile of v1, /device:TPU:1, one launch (start us, length us, event | category | flops | bytes accessed | tf_op | source)
XLA Modules:
  0.0 166.0 jit_solution(260395612074870186)
XLA Ops:
  0.6 0.0 copy-start
  0.6 1.6 copy-done
  2.2 0.8 shard_map.30
  3.0 10.1 %all-to-all-start = ((f32[16,2,4,128]{3,2,1,0:T(4,128)}), f32[16,2,4,128]{3,2,1,0:T(4,128)S(1)}, u32[]{:S(2)}, u32[]{:S(2)}) async-start(f32[16,2,4,128]{3,2,1,0:T(4,128)} %get-tuple-element.42), calls=%async_computation | async-start | bytes 131072 | tf_op jit(solution)/shard_map/all_to_all | solution.py:369
  13.2 0.1 pad_add_fusion.ids_ref.refs_0_
  13.2 7.7 %all-to-all-done.recv_ref = f32[16,2,4,128]{3,2,1,0:T(4,128)S(1)} async-done(((f32[16,2,4,128]{3,2,1,0:T(4,128)}), f32[16,2,4,128]{3,2,1,0:T(4,128)S(1)}, u32[]{:S(2)}, u32[]{:S(2)}) %all-to-all-start) | async-done | bytes 65568 | tf_op jit(solution)/shard_map/all_to_all | solution.py:369
  21.0 0.9 shard_map.31
  21.8 22.9 %all_to_all.50.refs_2_ = f32[32,4,4,128]{3,2,1,0:T(4,128)S(1)} all-to-all(f32[32,4,4,128]{3,2,1,0:T(4,128)S(1)} %get-tuple-element.43), channel_id=1, replica_groups=mesh['row'=32,'col'=16] {'row'}, dimensions={0} | all-to-all | bytes 524288 | tf_op jit(solution)/shard_map/all_to_all | solution.py:369
  44.8 0.9 shard_map.32
  45.7 13.8 %all_to_all.51.refs_2_ = f32[16,4,4,128]{3,2,1,0:T(4,128)S(1)} all-to-all(f32[16,4,4,128]{3,2,1,0:T(4,128)S(1)} %get-tuple-element.45), channel_id=1, replica_groups=mesh['row'=32,'col'=16] {'col'}, dimensions={0} | all-to-all | bytes 262144 | tf_op jit(solution)/shard_map/all_to_all | solution.py:369
  59.4 1.1 shard_map.33
  60.5 15.6 %all_to_all.52.refs_2_ = f32[32,4,4,128]{3,2,1,0:T(4,128)S(1)} all-to-all(f32[32,4,4,128]{3,2,1,0:T(4,128)S(1)} %get-tuple-element.49), channel_id=1, replica_groups=mesh['row'=32,'col'=16] {'row'}, dimensions={0} | all-to-all | bytes 524288 | tf_op jit(solution)/shard_map/all_to_all | solution.py:369
  76.1 1.0 shard_map.34
  77.1 12.3 %all_to_all.53.refs_2_ = f32[16,3,4,128]{3,2,1,0:T(4,128)S(1)} all-to-all(f32[16,3,4,128]{3,2,1,0:T(4,128)S(1)} %get-tuple-element.53), channel_id=1, replica_groups=mesh['row'=32,'col'=16] {'col'}, dimensions={0} | all-to-all | bytes 196608 | tf_op jit(solution)/shard_map/all_to_all | solution.py:369
  89.5 1.1 shard_map.35
  90.6 14.1 %all_to_all.54.refs_2_ = f32[32,3,4,128]{3,2,1,0:T(4,128)S(1)} all-to-all(f32[32,3,4,128]{3,2,1,0:T(4,128)S(1)} %get-tuple-element.57), channel_id=1, replica_groups=mesh['row'=32,'col'=16] {'row'}, dimensions={0} | all-to-all | bytes 393216 | tf_op jit(solution)/shard_map/all_to_all | solution.py:369
  104.7 1.0 shard_map.36
  105.8 12.9 %all_to_all.55.refs_2_ = f32[16,3,4,128]{3,2,1,0:T(4,128)S(1)} all-to-all(f32[16,3,4,128]{3,2,1,0:T(4,128)S(1)} %get-tuple-element.61), channel_id=1, replica_groups=mesh['row'=32,'col'=16] {'col'}, dimensions={0} | all-to-all | bytes 196608 | tf_op jit(solution)/shard_map/all_to_all | solution.py:369
  118.7 1.1 shard_map.37
  119.9 13.8 %all_to_all.56.refs_2_ = f32[32,3,4,128]{3,2,1,0:T(4,128)S(1)} all-to-all(f32[32,3,4,128]{3,2,1,0:T(4,128)S(1)} %get-tuple-element.65), channel_id=1, replica_groups=mesh['row'=32,'col'=16] {'row'}, dimensions={0} | all-to-all | bytes 393216 | tf_op jit(solution)/shard_map/all_to_all | solution.py:369
  133.7 1.1 shard_map.38
  134.7 12.9 %all_to_all.57.recv_ref.refs_1_ = f32[16,3,4,128]{3,2,1,0:T(4,128)S(1)} all-to-all(f32[16,3,4,128]{3,2,1,0:T(4,128)S(1)} %get-tuple-element.69), channel_id=1, replica_groups=mesh['row'=32,'col'=16] {'col'}, dimensions={0} | all-to-all | bytes 196608 | tf_op jit(solution)/shard_map/all_to_all | solution.py:369
  147.7 0.7 shard_map.39
  148.3 3.9 %all-to-all-start.9 = ((f32[32,1,4,128]{3,2,1,0:T(4,128)}), f32[32,1,4,128]{3,2,1,0:T(4,128)S(1)}, u32[]{:S(2)}, u32[]{:S(2)}) async-start(f32[32,1,4,128]{3,2,1,0:T(4,128)} %shard_map.39), calls=%async_computation.9 | async-start | bytes 131072 | tf_op jit(solution)/shard_map/all_to_all | solution.py:369
  152.2 1.7 %shard_map.40 = (f32[128,128]{1,0:T(8,128)S(1)}, f32[128,128]{1,0:T(8,128)S(1)}, f32[16,128]{1,0:T(8,128)S(1)}, f32[8,128]{1,0:T(8,128)S(1)}, f32[8,512]{1,0:T(8,128)S(1)}) custom-call(s32[2]{0:T(128)S(1)} %pad_add_fusion.ids_ref.refs_0_, f32[16,3,4,128]{3,2,1,0:T(4,128)S(1)} %all_to_all.57.recv_ref.refs_1_, ...), custom_call_target="tpu_custom_call" | custom-call | flops 40000000 | bytes 1000 | tf_op jit(solution)/shard_map/pallas_call | solution.py:357
  153.9 0.6 copy.3
  154.5 6.9 %all-to-all-done.9.refs_2_ = f32[32,1,4,128]{3,2,1,0:T(4,128)S(1)} async-done(((f32[32,1,4,128]{3,2,1,0:T(4,128)}), f32[32,1,4,128]{3,2,1,0:T(4,128)S(1)}, u32[]{:S(2)}, u32[]{:S(2)}) %all-to-all-start.9) | async-done | bytes 65568 | tf_op jit(solution)/shard_map/all_to_all | solution.py:369
  161.4 4.6 %shard_map.41 = f32[512,1024]{1,0:T(8,128)} custom-call(s32[2]{0:T(128)S(1)} %pad_add_fusion.ids_ref.refs_0_, f32[512,1024]{1,0:T(8,128)S(1)} %get-tuple-element.41.a_ref.refs_1_, f32[32,1,4,128]{3,2,1,0:T(4,128)S(1)} %all-to-all-done.9.refs_2_, f32[4,128]{1,0:T(4,128)S(1)} %get-tuple-element.46.refs_3_, f32[32,128]{1,0:T(8,128)S(1)} %get-tuple-element.70.refs_4_, ...), custom_call_target="tpu_custom_call" | custom-call | flops 1000 | bytes 1000 | tf_op jit(solution)/shard_map/pallas_call | solution.py:357
Async XLA Ops:
  0.6 1.6 copy-start
  3.0 18.0 %all-to-all-start = ((f32[16,2,4,128]{3,2,1,0:T(4,128)}), f32[16,2,4,128]{3,2,1,0:T(4,128)S(1)}, u32[]{:S(2)}, u32[]{:S(2)}) async-start(f32[16,2,4,128]{3,2,1,0:T(4,128)} %get-tuple-element.42), calls=%async_computation | async-start | bytes 131072 | tf_op jit(solution)/shard_map/all_to_all | solution.py:369
  148.3 13.1 %all-to-all-start.9 = ((f32[32,1,4,128]{3,2,1,0:T(4,128)}), f32[32,1,4,128]{3,2,1,0:T(4,128)S(1)}, u32[]{:S(2)}, u32[]{:S(2)}) async-start(f32[32,1,4,128]{3,2,1,0:T(4,128)} %shard_map.39), calls=%async_computation.9 | async-start | bytes 131072 | tf_op jit(solution)/shard_map/all_to_all | solution.py:369

commit v2 on v1

--- a/solution.py
+++ b/solution.py
@@ -14,6 +14,10 @@
 F32 = jnp.float32
 VMEM = pltpu.VMEM
 LIMIT = 16 << 20
+
+
+def places():
+    return lax.axis_index("row"), lax.axis_index("col")
 
 
 def total(x):
@@ -83,11 +87,13 @@
     )
 
 
-def start_kernel(a_ref, held_ref, send_ref):
-    held_ref[...] = a_ref[...]
-    left = [a_ref[q * LANES : (q + 1) * LANES, 0:LANES].T for q in range(4)]
+def start_kernel(a_ref, send_ref, slab_ref, sem):
+    copy = pltpu.make_async_copy(a_ref.at[:, pl.ds(0, LANES)], slab_ref, sem)
+    copy.start()
+    copy.wait()
+    left = [slab_ref[q * LANES : (q + 1) * LANES, :].T for q in range(4)]
     column = jnp.concatenate([x[0:1] for x in left], axis=0)
-    corner = a_ref[0:16, 0:LANES]
+    corner = slab_ref[0:16, :]
     packed = jnp.zeros((1, LANES), F32)
     for j in range(COLS):
         lanes = iota((1, LANES), 1)
@@ -101,7 +107,8 @@
         send_ref[member, 1] = jnp.concatenate([*rows, packed, blank], axis=0)
 
 
-def first_kernel(ids_ref, a_ref, recv_ref, send_ref, piece_ref):
+def first_kernel(a_ref, recv_ref, send_ref, piece_ref):
+    ids_ref = places()
     column = recv_ref[0, 0]
     piece_ref[...] = recv_ref[0, 1]
     packed = recv_ref[0, 1][2:3]
@@ -154,8 +161,9 @@
 
 def step_kernel(step, *refs):
     refs = list(refs)
-    ids_ref, a_ref, recv_ref = refs[:3]
-    del refs[:3]
+    a_ref, recv_ref = refs[:2]
+    del refs[:2]
+    ids_ref = places()
     piece_ref = refs.pop(0) if step in (2, 3) else None
     scal = refs.pop(0)[...] if step > 2 else None
     q_refs = {i: refs.pop(0) for i in range(1, step - 1)}
@@ -242,7 +250,9 @@
 
 def panel_kernel(*refs):
     refs = list(refs)
-    ids_ref, recv_ref = refs[:2]
+    ids_ref = places()
+    refs.insert(0, None)
+    recv_ref = refs[1]
     scal_refs = {i: refs[1 + i] for i in range(1, 8)}
     q_refs = {i: refs[8 + i] for i in range(1, 8)}
     aq_refs = {i: refs[15 + i] for i in range(1, 7)}
@@ -285,7 +295,9 @@
 
 def trailing_kernel(*refs):
     refs = list(refs)
-    ids_ref, a_ref, recv_ref, packed_ref, edge_r_ref, edge_c_ref, factor_ref = refs[:7]
+    ids_ref = places()
+    refs.insert(0, None)
+    a_ref, recv_ref, packed_ref, edge_r_ref, edge_c_ref, factor_ref = refs[1:7]
     scal_refs = {i: refs[6 + i] for i in range(1, 9)}
     q_refs = {i: refs[14 + i] for i in range(1, 9)}
     aq_refs = {i: refs[22 + i] for i in range(1, 8)}
@@ -351,13 +363,10 @@
 
 
 def call(kernel, outs, *args, scratch=(), pinned=True, flops=1000):
-    def spec(x):
-        return pl.BlockSpec(memory_space=pltpu.SMEM if x.dtype == jnp.int32 else VMEM)
-
     return pl.pallas_call(
         kernel,
         out_shape=[VMEM(s, F32) if pinned else jax.ShapeDtypeStruct(s, F32) for s in outs],
-        in_specs=[spec(x) for x in args],
+        in_specs=[pl.BlockSpec(memory_space=VMEM)] * len(args),
         out_specs=[pl.BlockSpec(memory_space=VMEM)] * len(outs),
         scratch_shapes=[VMEM(s, F32) for s in scratch],
         compiler_params=pltpu.CompilerParams(vmem_limit_bytes=LIMIT),
@@ -370,15 +379,22 @@
 
 
 def local(matrix):
-    ids = jnp.stack([lax.axis_index("row"), lax.axis_index("col")]).astype(jnp.int32)
     whole = (N // LANES, LANES)
-    held, send = call(start_kernel, [matrix.shape, (16, 2, 4, LANES)], matrix)
+    send = pl.pallas_call(
+        start_kernel,
+        out_shape=VMEM((16, 2, 4, LANES), F32),
+        in_specs=[pl.BlockSpec(memory_space=pltpu.HBM)],
+        out_specs=pl.BlockSpec(memory_space=VMEM),
+        scratch_shapes=[VMEM((matrix.shape[0], LANES), F32), pltpu.SemaphoreType.DMA],
+        compiler_params=pltpu.CompilerParams(vmem_limit_bytes=LIMIT),
+    )(pltpu.with_memory_space_constraint(matrix, pltpu.HBM))
+    held = matrix
     recv = exchange(send, "col")
-    send, piece = call(first_kernel, [(32, 4, 4, LANES), (4, LANES)], ids, held, recv)
+    send, piece = call(first_kernel, [(32, 4, 4, LANES), (4, LANES)], held, recv)
     recv = exchange(send, "row")
     qs, aqs, scals = {}, {}, {}
     for step in range(2, 9):
-        args = [ids, held, recv]
+        args = [held, recv]
         if step in (2, 3):
             args.append(piece)
         if step > 2:
@@ -411,7 +427,6 @@
     qs[8], aqs[7], scals[8], factor, reflect = call(
         panel_kernel,
         [whole, whole, (16, LANES), (8, LANES), (8, matrix.shape[0])],
-        ids,
         recv,
         *[scals[i] for i in range(1, 8)],
         *[qs[i] for i in range(1, 8)],
@@ -421,7 +436,6 @@
     (trailing,) = call(
         trailing_kernel,
         [matrix.shape],
-        ids,
         held,
         last,
         packed,

time: 167 us -> 160 us (0.958)
  blocking collectives: 118 us -> 136 us
  starting transfers between devices: 14 us -> 3.85 us
  waiting for transfers between devices: 14.7 us -> 7.48 us
  Pallas kernels: 15.8 us -> 10.9 us
    all_to_all x8 -> x9, blocking collectives: 118 us -> 136 us  [exchange(): return lax.all_to_all(x, axis, 0, 0, tiled=True)]
    all_to_all x2 -> x1, starting transfers between devices: 14 us -> 3.85 us  [exchange(): return lax.all_to_all(x, axis, 0, 0, tiled=True)]
    all_to_all x2 -> x1, waiting for transfers between devices: 14.7 us -> 7.48 us  [exchange(): return lax.all_to_all(x, axis, 0, 0, tiled=True)]
    pallas_call x12 -> x11, Pallas kernels: 15.8 us -> 9.66 us  [call(): pl.pallas_call(kernel, out_shape=[VMEM(s, F32) if pinned else jax.ShapeDt...]
  transfers between devices with their start and end apart: 2 -> 1, of which waited for: 2 -> 1; matrix products, arithmetic and copies ran while one was open for 0% -> 0% of each run, Pallas kernels for 1% -> 1%
where the time goes in v2:
time: 160 us
  blocking collectives  136 us (85%)
  Pallas kernels  10.9 us (7%)
  waiting for transfers between devices  7.48 us (5%)
  starting transfers between devices  3.85 us (2%)
    all_to_all x9, blocking collectives, exchange(): return lax.all_to_all(x, axis, 0, 0, tiled=True)  136 us
    pallas_call x11, Pallas kernels, call(): pl.pallas_call(kernel, out_shape=[VMEM(s, F32) if pinned else jax.ShapeDt...  9.66 us
    all_to_all x1, waiting for transfers between devices, exchange(): return lax.all_to_all(x, axis, 0, 0, tiled=True)  7.48 us
    all_to_all x1, starting transfers between devices, exchange(): return lax.all_to_all(x, axis, 0, 0, tiled=True)  3.85 us
  transfers between devices with their start and end apart: 1, of which 1 were waited for; matrix products, arithmetic and copies ran while one was open for 0% of the time, Pallas kernels for 1%

profile of v2, /device:TPU:1, one launch (start us, length us, event | category | flops | bytes accessed | tf_op | source)
XLA Modules:
  0.0 159.8 jit_solution(7659964352418209143)
XLA Ops:
  0.6 0.0 copy-start
  0.6 1.3 shard_map.30
  1.9 17.1 %all_to_all.50.recv_ref = f32[16,2,4,128]{3,2,1,0:T(4,128)S(1)} all-to-all(f32[16,2,4,128]{3,2,1,0:T(4,128)S(1)} %shard_map.30), channel_id=1, replica_groups=mesh['row'=32,'col'=16] {'col'}, dimensions={0} | all-to-all | bytes 131072 | tf_op jit(solution)/shard_map/all_to_all | solution.py:378
  19.0 0.0 copy-done
  19.0 0.3 shard_map.31
  19.3 23.6 %all_to_all.51.refs_1_ = f32[32,4,4,128]{3,2,1,0:T(4,128)S(1)} all-to-all(f32[32,4,4,128]{3,2,1,0:T(4,128)S(1)} %get-tuple-element.39), channel_id=1, replica_groups=mesh['row'=32,'col'=16] {'row'}, dimensions={0} | all-to-all | bytes 524288 | tf_op jit(solution)/shard_map/all_to_all | solution.py:378
  42.9 0.3 shard_map.32
  43.2 13.8 %all_to_all.52.refs_1_ = f32[16,4,4,128]{3,2,1,0:T(4,128)S(1)} all-to-all(f32[16,4,4,128]{3,2,1,0:T(4,128)S(1)} %get-tuple-element.41), channel_id=1, replica_groups=mesh['row'=32,'col'=16] {'col'}, dimensions={0} | all-to-all | bytes 262144 | tf_op jit(solution)/shard_map/all_to_all | solution.py:378
  57.0 0.6 shard_map.33
  57.6 15.6 %all_to_all.53.refs_1_ = f32[32,4,4,128]{3,2,1,0:T(4,128)S(1)} all-to-all(f32[32,4,4,128]{3,2,1,0:T(4,128)S(1)} %get-tuple-element.45), channel_id=1, replica_groups=mesh['row'=32,'col'=16] {'row'}, dimensions={0} | all-to-all | bytes 524288 | tf_op jit(solution)/shard_map/all_to_all | solution.py:378
  73.2 0.5 shard_map.34
  73.7 12.3 %all_to_all.54.refs_1_ = f32[16,3,4,128]{3,2,1,0:T(4,128)S(1)} all-to-all(f32[16,3,4,128]{3,2,1,0:T(4,128)S(1)} %get-tuple-element.49), channel_id=1, replica_groups=mesh['row'=32,'col'=16] {'col'}, dimensions={0} | all-to-all | bytes 196608 | tf_op jit(solution)/shard_map/all_to_all | solution.py:378
  86.0 0.6 shard_map.35
  86.6 14.1 %all_to_all.55.refs_1_ = f32[32,3,4,128]{3,2,1,0:T(4,128)S(1)} all-to-all(f32[32,3,4,128]{3,2,1,0:T(4,128)S(1)} %get-tuple-element.53), channel_id=1, replica_groups=mesh['row'=32,'col'=16] {'row'}, dimensions={0} | all-to-all | bytes 393216 | tf_op jit(solution)/shard_map/all_to_all | solution.py:378
  100.7 0.5 shard_map.36
  101.2 12.9 %all_to_all.56.refs_1_ = f32[16,3,4,128]{3,2,1,0:T(4,128)S(1)} all-to-all(f32[16,3,4,128]{3,2,1,0:T(4,128)S(1)} %get-tuple-element.57), channel_id=1, replica_groups=mesh['row'=32,'col'=16] {'col'}, dimensions={0} | all-to-all | bytes 196608 | tf_op jit(solution)/shard_map/all_to_all | solution.py:378
  114.2 0.6 shard_map.37
  114.8 13.8 %all_to_all.57.refs_1_ = f32[32,3,4,128]{3,2,1,0:T(4,128)S(1)} all-to-all(f32[32,3,4,128]{3,2,1,0:T(4,128)S(1)} %get-tuple-element.61), channel_id=1, replica_groups=mesh['row'=32,'col'=16] {'row'}, dimensions={0} | all-to-all | bytes 393216 | tf_op jit(solution)/shard_map/all_to_all | solution.py:378
  128.6 0.5 shard_map.38
  129.1 12.9 %all_to_all.58.recv_ref.refs_0_ = f32[16,3,4,128]{3,2,1,0:T(4,128)S(1)} all-to-all(f32[16,3,4,128]{3,2,1,0:T(4,128)S(1)} %get-tuple-element.65), channel_id=1, replica_groups=mesh['row'=32,'col'=16] {'col'}, dimensions={0} | all-to-all | bytes 196608 | tf_op jit(solution)/shard_map/all_to_all | solution.py:378
  142.0 0.7 shard_map.39
  142.7 3.9 %all-to-all-start.9 = ((f32[32,1,4,128]{3,2,1,0:T(4,128)}), f32[32,1,4,128]{3,2,1,0:T(4,128)S(1)}, u32[]{:S(2)}, u32[]{:S(2)}) async-start(f32[32,1,4,128]{3,2,1,0:T(4,128)} %shard_map.39), calls=%async_computation.9 | async-start | bytes 131072 | tf_op jit(solution)/shard_map/all_to_all | solution.py:378
  146.6 1.1 shard_map.40
  147.7 0.6 copy.3
  148.3 7.5 %all-to-all-done.9.refs_1_ = f32[32,1,4,128]{3,2,1,0:T(4,128)S(1)} async-done(((f32[32,1,4,128]{3,2,1,0:T(4,128)}), f32[32,1,4,128]{3,2,1,0:T(4,128)S(1)}, u32[]{:S(2)}, u32[]{:S(2)}) %all-to-all-start.9) | async-done | bytes 65568 | tf_op jit(solution)/shard_map/all_to_all | solution.py:378
  155.8 4.0 %shard_map.41 = f32[512,1024]{1,0:T(8,128)} custom-call(f32[512,1024]{1,0:T(8,128)S(1)} %copy-done, f32[32,1,4,128]{3,2,1,0:T(4,128)S(1)} %all-to-all-done.9.refs_1_, f32[4,128]{1,0:T(4,128)S(1)} %get-tuple-element.42.refs_2_, f32[32,128]{1,0:T(8,128)S(1)} %get-tuple-element.66.refs_3_, f32[64,128]{1,0:T(8,128)S(1)} %get-tuple-element.67.refs_4_, ...), custom_call_target="tpu_custom_call" | custom-call | flops 1000 | bytes 1000 | tf_op jit(solution)/shard_map/pallas_call | solution.py:366
Async XLA Ops:
  0.6 18.3 %copy-start = (f32[512,1024]{1,0:T(8,128)S(1)}, f32[512,1024]{1,0:T(8,128)}, u32[]{:S(2)}) copy-start(f32[512,1024]{1,0:T(8,128)} %refs_0_.15) | copy-start | bytes 6291460
  142.7 13.1 %all-to-all-start.9 = ((f32[32,1,4,128]{3,2,1,0:T(4,128)}), f32[32,1,4,128]{3,2,1,0:T(4,128)S(1)}, u32[]{:S(2)}, u32[]{:S(2)}) async-start(f32[32,1,4,128]{3,2,1,0:T(4,128)} %shard_map.39), calls=%async_computation.9 | async-start | bytes 131072 | tf_op jit(solution)/shard_map/all_to_all | solution.py:378

commit v3 on v2

--- a/solution.py
+++ b/solution.py
@@ -128,14 +128,14 @@
     return scal[k : k + 1, 0:1]
 
 
-def settle(step, y_whole, scal, qs, aqs):
+def settle(step, y_whole, scal, qs, previous):
     if step == 2:
         aq = None
         u = without_first(y_whole, None)
     else:
         aq = y_whole
-        for i in range(1, step - 2):
-            aq = aq - coefficient(scal, i) * aqs[i]
+        if step > 3:
+            aq = aq - coefficient(scal, step - 3) * previous
         aq = aq * coefficient(scal, 8)
         u = aq
         if step > 3:
@@ -159,6 +159,13 @@
     return aq, w * inverse, length, inverse, cs, jnp.concatenate(out, axis=0)
 
 
+def keep_rows(out_ref, ref):
+    row_index, col_index = places()
+    out_ref[0:4, :] = ref[pl.ds(4 * row_index, 4), :]
+    out_ref[4:12, :] = ref[pl.ds(8 * col_index, 8), :]
+    out_ref[12:13, :] = ref[0:1, :]
+
+
 def step_kernel(step, *refs):
     refs = list(refs)
     a_ref, recv_ref = refs[:2]
@@ -167,10 +174,11 @@
     piece_ref = refs.pop(0) if step in (2, 3) else None
     scal = refs.pop(0)[...] if step > 2 else None
     q_refs = {i: refs.pop(0) for i in range(1, step - 1)}
-    aq_refs = {i: refs.pop(0) for i in range(1, step - 2)}
+    previous_ref = refs.pop(0) if step > 3 else None
     send_ref = refs.pop(0)
     q_ref = refs.pop(0)
     aq_ref = refs.pop(0) if step > 2 else None
+    aq_rows_ref = refs.pop(0) if step > 2 else None
     scal_ref = refs.pop(0)
     edge_ref = refs.pop(0) if step in (3, 4) else None
     new_piece_ref = refs.pop(0) if step == 2 else None
@@ -189,17 +197,17 @@
         y_whole,
         scal,
         {i: r[...] for i, r in q_refs.items()},
-        {i: r[...] for i, r in aq_refs.items()},
+        previous_ref[...] if step > 3 else None,
     )
     q_ref[...] = q
     scal_ref[...] = scal_out
     if aq_ref is not None:
         aq_ref[...] = aq
+        keep_rows(aq_rows_ref, aq_ref)
     at = pl.ds(chunk * rows, rows)
     here = y_here
-    for i in cs:
-        source = aq_ref if i == step - 2 else aq_refs[i]
-        here = here - cs[i] * source[at, :]
+    if step > 2:
+        here = here - cs[step - 2] * aq_ref[at, :]
     here = here * inverse
     if step > 2:
         here = here - length * q_refs[step - 2][at, :]
@@ -239,7 +247,10 @@
 
 
 def rows_at(refs, row):
-    return jnp.concatenate([sign(k) * refs[k][pl.ds(row, 1), :] for k in range(1, 9)], axis=0)
+    blank = jnp.zeros((1, LANES), F32)
+    return jnp.concatenate(
+        [sign(k) * refs[k][pl.ds(row, 1), :] if k in refs else blank for k in range(1, 9)], axis=0
+    )
 
 
 def d_tile(q_refs, row):
@@ -248,27 +259,38 @@
     return unit - rows_at(q_refs, row)
 
 
+def three(x):
+    high = x.astype(jnp.bfloat16).astype(F32)
+    middle = (x - high).astype(jnp.bfloat16).astype(F32)
+    low = (x - high - middle).astype(jnp.bfloat16).astype(F32)
+    return high, middle, low
+
+
 def panel_kernel(*refs):
+    row_index, col_index = places()
     refs = list(refs)
-    ids_ref = places()
     refs.insert(0, None)
-    recv_ref = refs[1]
-    scal_refs = {i: refs[1 + i] for i in range(1, 8)}
-    q_refs = {i: refs[8 + i] for i in range(1, 8)}
-    aq_refs = {i: refs[15 + i] for i in range(1, 7)}
-    q_out, aq_out, scal_out, factor_ref, reflect_ref = refs[22:27]
+    recv_ref, packed_ref, edge_r_ref, edge_c_ref = refs[1:5]
+    scal_refs = {i: refs[4 + i] for i in range(1, 8)}
+    q_refs = {i: refs[11 + i] for i in range(1, 8)}
+    aq_rows = {i: refs[18 + i] for i in range(1, 7)}
+    previous_ref = refs[25]
+    q_out, rest_out, reflect_ref, side_ref, left_ref, right_ref, aq_out, rows_out = refs[26:34]
     y_whole = whole_from_cols(recv_ref, 1)
-    aq, q, _, _, _, scal = settle(
+    aq, q, _, _, cs, scal = settle(
         9,
         y_whole,
         scal_refs[7][...],
         {i: r[...] for i, r in q_refs.items()},
-        {i: r[...] for i, r in aq_refs.items()},
+        previous_ref[...],
     )
     q_out[...] = q
     aq_out[...] = aq
-    scal_out[...] = scal
+    side_ref[96:104, :] = scal[8:16]
     q_refs[8] = q_out
+    keep_rows(rows_out, aq_out)
+    aq_rows[7] = rows_out
+    rest_out[...] = cs[7] * aq
     lanes, ks = iota((8, LANES), 1), iota((8, LANES), 0)
     top = d_tile(q_refs, 0)
     work = jnp.where(lanes < 8, pltpu.roll(top, LANES - 1, 1), 0.0)
@@ -281,91 +303,116 @@
         row = row / row[:, k : k + 1]
         column = jnp.where(ks == k, 0.0, work)[:, k : k + 1]
         work = jnp.where(ks == k, row, work - column * row)
-    factor_ref[...] = jnp.where(lanes < 8, pltpu.roll(work, LANES - 8, 1), 0.0)
+    factor = pltpu.roll(work, LANES - 8, 1)[:, 0:8]
+    flipped = jnp.concatenate(
+        [jnp.where(lanes < 8, pltpu.roll(work, LANES - 8, 1), 0.0), jnp.zeros((LANES - 8, LANES), F32)],
+        axis=0,
+    ).T[0:8, 0:8]
     to_reflect = jnp.where(lanes < 8, pltpu.roll(to_reflect, LANES - 8, 1), 0.0)
-    for t in range(4):
-        row = 4 * ids_ref[0] + t
-        d = d_tile(q_refs, row)
-        out = jnp.zeros((8, LANES), F32)
-        for k in range(8):
-            out = out + to_reflect[:, k : k + 1] * d[k : k + 1, :]
-        out = jnp.where((row == 0) & (lanes <= ks), 0.0, out)
-        reflect_ref[:, t * LANES : (t + 1) * LANES] = out
-
-
-def trailing_kernel(*refs):
-    refs = list(refs)
-    ids_ref = places()
-    refs.insert(0, None)
-    a_ref, recv_ref, packed_ref, edge_r_ref, edge_c_ref, factor_ref = refs[1:7]
-    scal_refs = {i: refs[6 + i] for i in range(1, 9)}
-    q_refs = {i: refs[14 + i] for i in range(1, 9)}
-    aq_refs = {i: refs[22 + i] for i in range(1, 8)}
-    out_ref, last_ref, left_ref, right_ref = refs[30:34]
-    scal = scal_refs[8][...]
-    aq = whole_from_rows(recv_ref, 0)
-    for i in range(1, 8):
-        aq = aq - coefficient(scal, i) * aq_refs[i][...]
-    aq = aq * coefficient(scal, 8)
-    last_ref[...] = aq
-    aq_refs[8] = last_ref
-    lanes, ks = iota((8, LANES), 1), iota((8, LANES), 0)
-    factor = factor_ref[...]
     inner = jnp.zeros((8, LANES), F32)
     packed = packed_ref[2:3]
-    for j in range(8):
-        entry = pltpu.roll(packed, LANES - 16 * j, 1) if j else packed
-        inner = jnp.where(ks == j, entry, inner)
-    inner = jnp.where((lanes >= 1) & (lanes <= 8), inner, 0.0)
-    cross = rows_at(aq_refs, 0)
-    cross = jnp.where((lanes >= 1) & (lanes <= 8), cross, 0.0)
+    for k in range(8):
+        entry = pltpu.roll(packed, LANES - 16 * k, 1) if k else packed
+        inner = jnp.where(ks == k, entry, inner)
+    used = (lanes >= 1) & (lanes <= 8)
+    inner = jnp.where(used, inner, 0.0)
+    cross = jnp.where(used, rows_at(aq_rows, 12), 0.0)
     inner = pltpu.roll(inner - cross, LANES - 1, 1)
     cross = pltpu.roll(cross, LANES - 1, 1)
     square = jnp.concatenate([cross, jnp.zeros((LANES - 8, LANES), F32)], axis=0)
     inner = inner - square.T[0:8]
-    for k in range(1, 9):
-        if k < 8:
-            alpha = scal_refs[k + 1][k : k + 1, :]
-            beta = scal_refs[k + 1][0:1, :]
-            near = ((ks == k - 1) & (lanes == k)) | ((ks == k) & (lanes == k - 1))
-            inner = inner - jnp.where(near, beta, 0.0)
-        else:
-            alpha = total(q_refs[8][...] * aq)
-        inner = inner + jnp.where((ks == k - 1) & (lanes == k - 1), alpha, 0.0)
-    factor = factor[:, 0:8]
+    for k in range(1, 8):
+        source = scal if k == 7 else scal_refs[k + 1]
+        near = ((ks == k - 1) & (lanes == k)) | ((ks == k) & (lanes == k - 1))
+        inner = inner - jnp.where(near, source[0:1, :], 0.0)
+        inner = inner + jnp.where((ks == k - 1) & (lanes == k - 1), source[k : k + 1, :], 0.0)
     inner = inner[:, 0:8]
     core = product(factor, product(inner, factor))
 
-    def tiles(base, count, edge_ref):
+    def tiles(base, count, edge_ref, first, kept):
         ds, ys = [], []
         for t in range(count):
             row = base + t
             d = d_tile(q_refs, row)
             edge = jnp.concatenate(
-                [edge_ref[count * j + t : count * j + t + 1, :] for j in range(8)], axis=0
+                [edge_ref[count * k + t : count * k + t + 1, :] for k in range(8)], axis=0
             )
-            ad = edge - rows_at(aq_refs, row)
+            ad = edge - rows_at(aq_rows, kept + t)
             ds.append(d)
             ys.append(product(factor, ad) - 0.5 * product(core, d))
+            side_ref[first + 8 * t : first + 8 * t + 8, :] = product(flipped, d)
         return ds, ys
 
-    ds, ys = tiles(4 * ids_ref[0], 4, edge_r_ref)
+    ds, ys = tiles(4 * row_index, 4, edge_r_ref, 0, 0)
     for t in range(4):
-        left_ref[0:8, t * LANES : (t + 1) * LANES] = ds[t]
-        left_ref[8:16, t * LANES : (t + 1) * LANES] = ys[t]
-    ds, ys = tiles(8 * ids_ref[1], 8, edge_c_ref)
+        high, middle, low = three(jnp.concatenate([ds[t], ys[t]], axis=0))
+        stack = [high, high, middle, middle, high, low, jnp.zeros((32, LANES), F32)]
+        at = slice(t * LANES, (t + 1) * LANES)
+        left_ref[at, :] = jnp.concatenate(stack, axis=0).T.astype(jnp.bfloat16)
+        out = jnp.zeros((8, LANES), F32)
+        for k in range(8):
+            out = out + to_reflect[:, k : k + 1] * ds[t][k : k + 1, :]
+        out = jnp.where((4 * row_index + t == 0) & (lanes <= ks), 0.0, out)
+        reflect_ref[:, t * LANES : (t + 1) * LANES] = out
+    ds, ys = tiles(8 * col_index, 8, edge_c_ref, 32, 4)
     for t in range(8):
-        right_ref[0:8, t * LANES : (t + 1) * LANES] = ys[t]
-        right_ref[8:16, t * LANES : (t + 1) * LANES] = ds[t]
+        high, middle, low = three(jnp.concatenate([ys[t], ds[t]], axis=0))
+        stack = [high, middle, high, middle, low, high]
+        at = slice(t * LANES, (t + 1) * LANES)
+        right_ref[:, at] = jnp.concatenate(stack, axis=0).astype(jnp.bfloat16)
+
+
+def trailing_kernel(
+    a_ref, recv_ref, q_ref, rest_ref, side_ref, left_ref, right_ref, out_ref, last_ref, block_ref, sems,
+):
+    row_index, col_index = places()
+    aq = (whole_from_rows(recv_ref, 0) - rest_ref[...]) * coefficient(side_ref, 96)
+    last_ref[...] = aq
+    alpha = total(q_ref[...] * aq)
+    lanes = iota((1, LANES), 1)
+    shifted = pltpu.roll(aq[0:1, :], LANES - 1, 1)
+    added = jnp.where(lanes == 7, 0.5 * alpha, 0.0) - jnp.where(lanes < 8, shifted, 0.0)
+    added = jnp.concatenate([added, jnp.zeros((7, LANES), F32)], axis=0).T[0:8, 0:1]
+
+    def last(base, count, first):
+        return [
+            -last_ref[pl.ds(base + t, 1), :]
+            - jnp.sum(added * side_ref[first + 8 * t : first + 8 * t + 8, :], axis=0, keepdims=True)
+            for t in range(count)
+        ]
+
+    ws_r = last(4 * row_index, 4, 0)
+    ws_c = last(8 * col_index, 8, 32)
+    blank = jnp.zeros((6, LANES), F32)
+    copies = []
     for q in range(4):
         at = slice(q * LANES, (q + 1) * LANES)
-        out_ref[at, :] = a_ref[at, :] - product(left_ref[:, at], right_ref[...])
+        upright = jnp.concatenate([side_ref[8 * q + 7 : 8 * q + 8, :], ws_r[q], blank], axis=0).T
+        change = jnp.dot(left_ref[at, 0:96], right_ref[...], preferred_element_type=F32)
+        for t in range(8):
+            to = slice(t * LANES, (t + 1) * LANES)
+            block_ref[at, to] = (
+                a_ref[at, to]
+                - change[:, to]
+                - upright[:, 0:1] * ws_c[t]
+                - upright[:, 1:2] * side_ref[39 + 8 * t : 40 + 8 * t, :]
+            )
+        copy = pltpu.make_async_copy(block_ref.at[at, :], out_ref.at[at, :], sems.at[q])
+        copy.start()
+        copies.append(copy)
+    for copy in copies:
+        copy.wait()
 
 
 def call(kernel, outs, *args, scratch=(), pinned=True, flops=1000):
+    def shape(x):
+        if not isinstance(x, tuple):
+            return x
+        return VMEM(x, F32) if pinned else jax.ShapeDtypeStruct(x, F32)
+
     return pl.pallas_call(
         kernel,
-        out_shape=[VMEM(s, F32) if pinned else jax.ShapeDtypeStruct(s, F32) for s in outs],
+        out_shape=[shape(x) for x in outs],
         in_specs=[pl.BlockSpec(memory_space=VMEM)] * len(args),
         out_specs=[pl.BlockSpec(memory_space=VMEM)] * len(outs),
         scratch_shapes=[VMEM(s, F32) for s in scratch],
@@ -392,18 +439,20 @@
     recv = exchange(send, "col")
     send, piece = call(first_kernel, [(32, 4, 4, LANES), (4, LANES)], held, recv)
     recv = exchange(send, "row")
-    qs, aqs, scals = {}, {}, {}
+    qs, aq_rows, scals, previous = {}, {}, {}, None
     for step in range(2, 9):
         args = [held, recv]
         if step in (2, 3):
             args.append(piece)
         if step > 2:
             args.append(scals[step - 2])
-        args += [qs[i] for i in range(1, step - 1)] + [aqs[i] for i in range(1, step - 2)]
+        args += [qs[i] for i in range(1, step - 1)]
+        if step > 3:
+            args.append(previous)
         groups = 4 if step in (2, 3) else 3
         outs = [(16 if step % 2 == 0 else 32, groups, 4, LANES), whole]
         if step > 2:
-            outs.append(whole)
+            outs += [whole, (16, LANES)]
         outs.append((16, LANES))
         if step in (3, 4):
             outs.append((32 if step == 3 else 64, LANES))
@@ -413,7 +462,8 @@
         send = result.pop(0)
         qs[step - 1] = result.pop(0)
         if step > 2:
-            aqs[step - 2] = result.pop(0)
+            previous = result.pop(0)
+            aq_rows[step - 2] = result.pop(0)
         scals[step - 1] = result.pop(0)
         if step == 3:
             edge_r = result.pop(0)
@@ -424,30 +474,30 @@
         recv = exchange(send, "col" if step % 2 == 0 else "row")
     (send,) = call(last_send_kernel, [(32, 1, 4, LANES)], recv)
     last = exchange(send, "row")
-    qs[8], aqs[7], scals[8], factor, reflect = call(
+    rows, cols = matrix.shape
+    q, rest, reflect, side, left, right = call(
         panel_kernel,
-        [whole, whole, (16, LANES), (8, LANES), (8, matrix.shape[0])],
+        [whole, whole, (8, rows), (104, LANES)]
+        + [VMEM((rows, LANES), jnp.bfloat16), VMEM((96, cols), jnp.bfloat16)],
         recv,
-        *[scals[i] for i in range(1, 8)],
-        *[qs[i] for i in range(1, 8)],
-        *[aqs[i] for i in range(1, 7)],
-        flops=40000000,
-    )
-    (trailing,) = call(
-        trailing_kernel,
-        [matrix.shape],
-        held,
-        last,
         packed,
         edge_r,
         edge_c,
-        factor,
-        *[scals[i] for i in range(1, 9)],
-        *[qs[i] for i in range(1, 9)],
-        *[aqs[i] for i in range(1, 8)],
-        scratch=[whole, (16, 512), (16, 1024)],
-        pinned=False,
-    )
+        *[scals[i] for i in range(1, 8)],
+        *[qs[i] for i in range(1, 8)],
+        *[aq_rows[i] for i in range(1, 7)],
+        previous,
+        scratch=[whole, (16, LANES)],
+        flops=40000000,
+    )
+    trailing = pl.pallas_call(
+        trailing_kernel,
+        out_shape=jax.ShapeDtypeStruct(matrix.shape, F32),
+        in_specs=[pl.BlockSpec(memory_space=VMEM)] * 7,
+        out_specs=pl.BlockSpec(memory_space=pltpu.HBM),
+        scratch_shapes=[VMEM(whole, F32), VMEM(matrix.shape, F32), pltpu.SemaphoreType.DMA((4,))],
+        compiler_params=pltpu.CompilerParams(vmem_limit_bytes=LIMIT),
+    )(held, last, q, rest, side, left, right)
     return trailing, reflect.T
 
 

time: 160 us -> 159 us (level)
  no operation moved by 1% of the time
where the time goes in v3:
time: 159 us; the launch traced here: 158 us
  blocking collectives  136 us (86%)
  Pallas kernels  10.2 us (6%)
  waiting for transfers between devices  6.41 us (4%)
  starting transfers between devices  3.86 us (2%)
    all_to_all x9, blocking collectives, exchange(): return lax.all_to_all(x, axis, 0, 0, tiled=True)  136 us
    pallas_call x10, Pallas kernels, call(): pl.pallas_call(kernel, out_shape=[shape(x) for x in outs], in_specs=[pl.B...  6.67 us
    all_to_all x1, waiting for transfers between devices, exchange(): return lax.all_to_all(x, axis, 0, 0, tiled=True)  6.41 us
    all_to_all x1, starting transfers between devices, exchange(): return lax.all_to_all(x, axis, 0, 0, tiled=True)  3.86 us
  transfers between devices with their start and end apart: 1, of which 1 were waited for; matrix products, arithmetic and copies ran while one was open for 0% of the time, Pallas kernels for 1%

profile of v3, /device:TPU:1, one launch (start us, length us, event | category | flops | bytes accessed | tf_op | source)
XLA Modules:
  0.0 158.0 jit_solution(2698214425961271689)
XLA Ops:
  0.6 0.0 copy-start
  0.6 1.3 shard_map.30
  1.9 17.1 %all_to_all.50.recv_ref = f32[16,2,4,128]{3,2,1,0:T(4,128)S(1)} all-to-all(f32[16,2,4,128]{3,2,1,0:T(4,128)S(1)} %shard_map.30), channel_id=1, replica_groups=mesh['row'=32,'col'=16] {'col'}, dimensions={0} | all-to-all | bytes 131072 | tf_op jit(solution)/shard_map/all_to_all | solution.py:425
  19.0 0.0 copy-done
  19.0 0.3 shard_map.31
  19.3 23.6 %all_to_all.51.refs_1_ = f32[32,4,4,128]{3,2,1,0:T(4,128)S(1)} all-to-all(f32[32,4,4,128]{3,2,1,0:T(4,128)S(1)} %get-tuple-element.46), channel_id=1, replica_groups=mesh['row'=32,'col'=16] {'row'}, dimensions={0} | all-to-all | bytes 524288 | tf_op jit(solution)/shard_map/all_to_all | solution.py:425
  42.9 0.3 shard_map.32
  43.2 13.8 %all_to_all.52.refs_1_ = f32[16,4,4,128]{3,2,1,0:T(4,128)S(1)} all-to-all(f32[16,4,4,128]{3,2,1,0:T(4,128)S(1)} %get-tuple-element.48), channel_id=1, replica_groups=mesh['row'=32,'col'=16] {'col'}, dimensions={0} | all-to-all | bytes 262144 | tf_op jit(solution)/shard_map/all_to_all | solution.py:425
  57.0 0.5 shard_map.33
  57.5 15.6 %all_to_all.53.refs_1_ = f32[32,4,4,128]{3,2,1,0:T(4,128)S(1)} all-to-all(f32[32,4,4,128]{3,2,1,0:T(4,128)S(1)} %get-tuple-element.52), channel_id=1, replica_groups=mesh['row'=32,'col'=16] {'row'}, dimensions={0} | all-to-all | bytes 524288 | tf_op jit(solution)/shard_map/all_to_all | solution.py:425
  73.2 0.5 shard_map.34
  73.6 12.3 %all_to_all.54.refs_1_ = f32[16,3,4,128]{3,2,1,0:T(4,128)S(1)} all-to-all(f32[16,3,4,128]{3,2,1,0:T(4,128)S(1)} %get-tuple-element.56), channel_id=1, replica_groups=mesh['row'=32,'col'=16] {'col'}, dimensions={0} | all-to-all | bytes 196608 | tf_op jit(solution)/shard_map/all_to_all | solution.py:425
  86.0 0.6 shard_map.35
  86.6 14.1 %all_to_all.55.refs_1_ = f32[32,3,4,128]{3,2,1,0:T(4,128)S(1)} all-to-all(f32[32,3,4,128]{3,2,1,0:T(4,128)S(1)} %get-tuple-element.60), channel_id=1, replica_groups=mesh['row'=32,'col'=16] {'row'}, dimensions={0} | all-to-all | bytes 393216 | tf_op jit(solution)/shard_map/all_to_all | solution.py:425
  100.7 0.5 shard_map.36
  101.2 12.9 %all_to_all.56.refs_1_ = f32[16,3,4,128]{3,2,1,0:T(4,128)S(1)} all-to-all(f32[16,3,4,128]{3,2,1,0:T(4,128)S(1)} %get-tuple-element.64), channel_id=1, replica_groups=mesh['row'=32,'col'=16] {'col'}, dimensions={0} | all-to-all | bytes 196608 | tf_op jit(solution)/shard_map/all_to_all | solution.py:425
  114.2 0.6 shard_map.37
  114.7 13.8 %all_to_all.57.refs_1_ = f32[32,3,4,128]{3,2,1,0:T(4,128)S(1)} all-to-all(f32[32,3,4,128]{3,2,1,0:T(4,128)S(1)} %get-tuple-element.68), channel_id=1, replica_groups=mesh['row'=32,'col'=16] {'row'}, dimensions={0} | all-to-all | bytes 393216 | tf_op jit(solution)/shard_map/all_to_all | solution.py:425
  128.6 0.5 shard_map.38
  129.1 12.9 %all_to_all.58.recv_ref.refs_0_ = f32[16,3,4,128]{3,2,1,0:T(4,128)S(1)} all-to-all(f32[16,3,4,128]{3,2,1,0:T(4,128)S(1)} %get-tuple-element.72), channel_id=1, replica_groups=mesh['row'=32,'col'=16] {'col'}, dimensions={0} | all-to-all | bytes 196608 | tf_op jit(solution)/shard_map/all_to_all | solution.py:425
  142.0 0.7 shard_map.39
  142.7 3.9 %all-to-all-start.9 = ((f32[32,1,4,128]{3,2,1,0:T(4,128)}), f32[32,1,4,128]{3,2,1,0:T(4,128)S(1)}, u32[]{:S(2)}, u32[]{:S(2)}) async-start(f32[32,1,4,128]{3,2,1,0:T(4,128)} %shard_map.39), calls=%async_computation.9 | async-start | bytes 131072 | tf_op jit(solution)/shard_map/all_to_all | solution.py:425
  146.5 2.2 %shard_map.40 = (f32[128,128]{1,0:T(8,128)S(1)}, f32[128,128]{1,0:T(8,128)S(1)}, f32[8,512]{1,0:T(8,128)S(1)}, f32[104,128]{1,0:T(8,128)S(1)}, bf16[512,128]{1,0...) custom-call(f32[16,3,4,128]{3,2,1,0:T(4,128)S(1)} %all_to_all.58.recv_ref.refs_0_, ...), custom_call_target="tpu_custom_call" | custom-call | flops 40000000 | bytes 1000 | tf_op jit(solution)/shard_map/pallas_call | solution.py:413
  148.7 0.6 copy.3
  149.3 6.4 %all-to-all-done.9.recv_ref = f32[32,1,4,128]{3,2,1,0:T(4,128)S(1)} async-done(((f32[32,1,4,128]{3,2,1,0:T(4,128)}), f32[32,1,4,128]{3,2,1,0:T(4,128)S(1)}, u32[]{:S(2)}, u32[]{:S(2)}) %all-to-all-start.9) | async-done | bytes 65568 | tf_op jit(solution)/shard_map/all_to_all | solution.py:425
  155.7 2.3 %shard_map.41 = f32[512,1024]{1,0:T(8,128)} custom-call(f32[512,1024]{1,0:T(8,128)S(1)} %copy-done, f32[32,1,4,128]{3,2,1,0:T(4,128)S(1)} %all-to-all-done.9.recv_ref, f32[128,128]{1,0:T(8,128)S(1)} %get-tuple-element.84.q_ref, f32[128,128]{1,0:T(8,128)S(1)} %get-tuple-element.85.rest_ref, f32[104,128]{1,0:T(8,128)S(1)} %get-tuple-element.86.side_ref, ...), custom_call_target="tpu_custom_call" | custom-call | tf_op jit(solution)/shard_map/pallas_call | solution.py:493
Async XLA Ops:
  0.6 18.3 %copy-start = (f32[512,1024]{1,0:T(8,128)S(1)}, f32[512,1024]{1,0:T(8,128)}, u32[]{:S(2)}) copy-start(f32[512,1024]{1,0:T(8,128)} %a_ref.5) | copy-start | bytes 6291460
  142.7 13.1 %all-to-all-start.9 = ((f32[32,1,4,128]{3,2,1,0:T(4,128)}), f32[32,1,4,128]{3,2,1,0:T(4,128)S(1)}, u32[]{:S(2)}, u32[]{:S(2)}) async-start(f32[32,1,4,128]{3,2,1,0:T(4,128)} %shard_map.39), calls=%async_computation.9 | async-start | bytes 131072 | tf_op jit(solution)/shard_map/all_to_all | solution.py:425

commit v4 on v3

--- a/solution.py
+++ b/solution.py
@@ -14,6 +14,9 @@
 F32 = jnp.float32
 VMEM = pltpu.VMEM
 LIMIT = 16 << 20
+GUARD = False
+GROWTH = 16.0
+PIVOT = 0.05
 
 
 def places():
@@ -128,96 +131,109 @@
     return scal[k : k + 1, 0:1]
 
 
-def settle(step, y_whole, scal, qs, previous):
+def settle(step, given, scal, qs):
+    u = without_first(given, None) if step == 2 else given
+    zero = jnp.zeros((1, LANES), F32)
+    w, cs, growth = u, {}, zero + 1.0
     if step == 2:
-        aq = None
-        u = without_first(y_whole, None)
+        alpha = shift = given[0:1, 0:1]
     else:
-        aq = y_whole
-        if step > 3:
-            aq = aq - coefficient(scal, step - 3) * previous
-        aq = aq * coefficient(scal, 8)
-        u = aq
-        if step > 3:
-            u = u - coefficient(scal, 0) * qs[step - 3]
-        u = without_first(u, None)
-    known = range(1, step - 1)
-    rows = [jnp.sum(u * qs[i], axis=0, keepdims=True) for i in known]
-    w = u
-    cs = {}
-    if rows:
-        rows = rows + [jnp.zeros((1, LANES), F32)] * (8 - len(rows))
+        known = range(1, step - 1)
+        rows = [jnp.sum(u * qs[i], axis=0, keepdims=True) for i in known]
+        rows = rows + [zero] * (8 - len(rows))
         sums = jnp.sum(jnp.concatenate(rows, axis=0), axis=1, keepdims=True)
         for i in known:
             cs[i] = sums[i - 1 : i, 0:1]
             w = w - cs[i] * qs[i]
+        growth = jnp.sum(sums * sums, axis=0, keepdims=True)
+        alpha, before = cs[step - 2] + coefficient(scal, 9), coefficient(scal, 10)
+        smaller = jnp.where(jnp.abs(alpha) < jnp.abs(before), alpha, before)
+        shift = jnp.where(alpha * before > 0.0, smaller, 0.0)
     length = jnp.sqrt(total(w * w))
     inverse = 1.0 / length
-    zero = jnp.zeros((1, LANES), F32)
+    if step > 2:
+        growth = coefficient(scal, 11) * (1.0 + growth * inverse * inverse)
     out = [zero + length] + [zero + cs[i] if i in cs else zero for i in range(1, 8)]
-    out = out + [zero + inverse] + [zero] * 7
-    return aq, w * inverse, length, inverse, cs, jnp.concatenate(out, axis=0)
-
-
-def keep_rows(out_ref, ref):
+    out = out + [zero + x for x in (inverse, shift, alpha, growth)] + [zero] * 4
+    return w * inverse, length, inverse, shift, cs, jnp.concatenate(out, axis=0)
+
+
+def given_rows(recv_ref, by_rows):
     row_index, col_index = places()
-    out_ref[0:4, :] = ref[pl.ds(4 * row_index, 4), :]
-    out_ref[4:12, :] = ref[pl.ds(8 * col_index, 8), :]
-    out_ref[12:13, :] = ref[0:1, :]
+    if by_rows:
+        group = recv_ref.shape[1] - 1 if recv_ref.shape[1] < 3 else 2
+        here = recv_ref[row_index, group]
+        there = [recv_ref[2 * col_index + k, group] for k in range(2)]
+        first = recv_ref[0, group][0:1]
+    else:
+        here = recv_ref[row_index // 2, 1 + row_index % 2]
+        there = [recv_ref[col_index, 1 + k] for k in range(2)]
+        first = recv_ref[0, 1][0:1]
+    return jnp.concatenate([here, *there, first, jnp.zeros((3, LANES), F32)], axis=0)
+
+
+def kept_rows(ref):
+    row_index, col_index = places()
+    here, there = ref[pl.ds(4 * row_index, 4), :], ref[pl.ds(8 * col_index, 8), :]
+    return jnp.concatenate([here, there, ref[0:1, :], jnp.zeros((3, LANES), F32)], axis=0)
+
+
+def product_rows(step, recv_ref, scal, q_refs):
+    out = given_rows(recv_ref, step % 2 == 0)
+    out = out + coefficient(scal, 9) * kept_rows(q_refs[step - 2])
+    if step > 3:
+        return out + coefficient(scal, 0) * kept_rows(q_refs[step - 3])
+    row_index, col_index = places()
+    rows, lanes = iota(out.shape, 0), iota(out.shape, 1)
+    start = ((rows == 0) & (row_index == 0)) | ((rows == 4) & (col_index == 0)) | (rows == 12)
+    return out + jnp.where(start & (lanes == 0), coefficient(scal, 0), 0.0)
 
 
 def step_kernel(step, *refs):
     refs = list(refs)
     a_ref, recv_ref = refs[:2]
     del refs[:2]
-    ids_ref = places()
+    row_index, col_index = places()
     piece_ref = refs.pop(0) if step in (2, 3) else None
     scal = refs.pop(0)[...] if step > 2 else None
     q_refs = {i: refs.pop(0) for i in range(1, step - 1)}
-    previous_ref = refs.pop(0) if step > 3 else None
+    rows_refs = {i: refs.pop(0) for i in range(1, step - 2)}
     send_ref = refs.pop(0)
     q_ref = refs.pop(0)
-    aq_ref = refs.pop(0) if step > 2 else None
-    aq_rows_ref = refs.pop(0) if step > 2 else None
+    if step > 2:
+        rows_refs[step - 2] = refs.pop(0)
     scal_ref = refs.pop(0)
     edge_ref = refs.pop(0) if step in (3, 4) else None
     new_piece_ref = refs.pop(0) if step == 2 else None
 
     even = step % 2 == 0
     if even:
-        y_here = along_cols(recv_ref)
-        y_whole = whole_from_rows(recv_ref, 2)
-        chunk, rows = ids_ref[1], 8
+        y_here, given = along_cols(recv_ref), whole_from_rows(recv_ref, 2)
+        chunk, count, part = col_index, 8, slice(4, 12)
     else:
-        y_here = along_rows(recv_ref)
-        y_whole = whole_from_cols(recv_ref, 1)
-        chunk, rows = ids_ref[0], 4
-    aq, q, length, inverse, cs, scal_out = settle(
-        step,
-        y_whole,
-        scal,
-        {i: r[...] for i, r in q_refs.items()},
-        previous_ref[...] if step > 3 else None,
+        y_here, given = along_rows(recv_ref), whole_from_cols(recv_ref, 1)
+        chunk, count, part = row_index, 4, slice(0, 4)
+    if step > 2:
+        rows_refs[step - 2][...] = product_rows(step, recv_ref, scal, q_refs)
+    q, length, inverse, shift, cs, scal_out = settle(
+        step, given, scal, {i: r[...] for i, r in q_refs.items()}
     )
     q_ref[...] = q
     scal_ref[...] = scal_out
-    if aq_ref is not None:
-        aq_ref[...] = aq
-        keep_rows(aq_rows_ref, aq_ref)
-    at = pl.ds(chunk * rows, rows)
+    at = pl.ds(chunk * count, count)
     here = y_here
-    if step > 2:
-        here = here - cs[step - 2] * aq_ref[at, :]
-    here = here * inverse
+    for i in cs:
+        here = here - cs[i] * rows_refs[i][part, :]
+    here = here * inverse - shift * q_ref[at, :]
     if step > 2:
         here = here - length * q_refs[step - 2][at, :]
     here = without_first(here, chunk)
     if even:
         send_all(send_ref, 0, [times_cols(a_ref, here)])
-        send_all(send_ref, 1, halves(y_here))
+        send_all(send_ref, 1, halves(here))
     else:
         send_all(send_ref, 0, halves(times_rows(a_ref, here)))
-        send_all(send_ref, 2, [y_here])
+        send_all(send_ref, 2, [here])
     if step in (2, 3):
         send_all(send_ref, 3, [piece_ref[...]])
     if step == 2:
@@ -274,35 +290,36 @@
     scal_refs = {i: refs[4 + i] for i in range(1, 8)}
     q_refs = {i: refs[11 + i] for i in range(1, 8)}
     aq_rows = {i: refs[18 + i] for i in range(1, 7)}
-    previous_ref = refs[25]
-    q_out, rest_out, reflect_ref, side_ref, left_ref, right_ref, aq_out, rows_out = refs[26:34]
-    y_whole = whole_from_cols(recv_ref, 1)
-    aq, q, _, _, cs, scal = settle(
-        9,
-        y_whole,
-        scal_refs[7][...],
-        {i: r[...] for i, r in q_refs.items()},
-        previous_ref[...],
+    q_out, flag_ref, reflect_ref, side_ref, left_ref, right_ref, rows_out = refs[25:32]
+    q, length, _, _, cs, scal = settle(
+        9, whole_from_cols(recv_ref, 1), scal_refs[7][...], {i: r[...] for i, r in q_refs.items()}
     )
     q_out[...] = q
-    aq_out[...] = aq
+    rows_out[...] = product_rows(9, recv_ref, scal_refs[7][...], q_refs)
+    aq_rows[7] = rows_out
+    rest = jnp.zeros((16, LANES), F32)
+    for i in range(1, 8):
+        rest = rest + cs[i] * aq_rows[i][...]
     side_ref[96:104, :] = scal[8:16]
+    side_ref[104:120, :] = rest
+    side_ref[120:128, :] = jnp.zeros((8, LANES), F32) + cs[7] * length
     q_refs[8] = q_out
-    keep_rows(rows_out, aq_out)
-    aq_rows[7] = rows_out
-    rest_out[...] = cs[7] * aq
     lanes, ks = iota((8, LANES), 1), iota((8, LANES), 0)
     top = d_tile(q_refs, 0)
     work = jnp.where(lanes < 8, pltpu.roll(top, LANES - 1, 1), 0.0)
     work = work + jnp.where(lanes == ks + 8, 1.0, 0.0)
     to_reflect = jnp.zeros((8, LANES), F32)
+    pivot = jnp.ones((1, 1), F32)
     for k in range(8):
         row = work[k : k + 1]
+        pivot = jnp.minimum(pivot, row[:, k : k + 1])
         beta = (scal if k == 7 else scal_refs[k + 1])[0:1, :]
         to_reflect = jnp.where(ks == k, row * beta, to_reflect)
         row = row / row[:, k : k + 1]
         column = jnp.where(ks == k, 0.0, work)[:, k : k + 1]
         work = jnp.where(ks == k, row, work - column * row)
+    sound = (scal[11:12, 0:1] <= GROWTH) & (pivot >= PIVOT)
+    flag_ref[...] = jnp.zeros((8, LANES), F32) + jnp.where(sound, 1.0, 0.0)
     factor = pltpu.roll(work, LANES - 8, 1)[:, 0:8]
     flipped = jnp.concatenate(
         [jnp.where(lanes < 8, pltpu.roll(work, LANES - 8, 1), 0.0), jnp.zeros((LANES - 8, LANES), F32)],
@@ -325,7 +342,8 @@
         source = scal if k == 7 else scal_refs[k + 1]
         near = ((ks == k - 1) & (lanes == k)) | ((ks == k) & (lanes == k - 1))
         inner = inner - jnp.where(near, source[0:1, :], 0.0)
-        inner = inner + jnp.where((ks == k - 1) & (lanes == k - 1), source[k : k + 1, :], 0.0)
+        alpha = source[10:11, :]
+        inner = inner + jnp.where((ks == k - 1) & (lanes == k - 1), alpha, 0.0)
     inner = inner[:, 0:8]
     core = product(factor, product(inner, factor))
 
@@ -363,26 +381,26 @@
 
 
 def trailing_kernel(
-    a_ref, recv_ref, q_ref, rest_ref, side_ref, left_ref, right_ref, out_ref, last_ref, block_ref, sems,
+    a_ref, recv_ref, q_ref, side_ref, left_ref, right_ref, out_ref, block_ref, sems
 ):
-    row_index, col_index = places()
-    aq = (whole_from_rows(recv_ref, 0) - rest_ref[...]) * coefficient(side_ref, 96)
-    last_ref[...] = aq
-    alpha = total(q_ref[...] * aq)
+    inverse = coefficient(side_ref, 96)
+    aq = (given_rows(recv_ref, True) - side_ref[104:120, :]) * inverse
+    alpha = total(q_ref[...] * whole_from_rows(recv_ref, 0)) - coefficient(side_ref, 120)
+    alpha = alpha * inverse
     lanes = iota((1, LANES), 1)
-    shifted = pltpu.roll(aq[0:1, :], LANES - 1, 1)
+    shifted = pltpu.roll(aq[12:13, :], LANES - 1, 1)
     added = jnp.where(lanes == 7, 0.5 * alpha, 0.0) - jnp.where(lanes < 8, shifted, 0.0)
     added = jnp.concatenate([added, jnp.zeros((7, LANES), F32)], axis=0).T[0:8, 0:1]
 
-    def last(base, count, first):
+    def last(count, first, kept):
         return [
-            -last_ref[pl.ds(base + t, 1), :]
+            -aq[kept + t : kept + t + 1, :]
             - jnp.sum(added * side_ref[first + 8 * t : first + 8 * t + 8, :], axis=0, keepdims=True)
             for t in range(count)
         ]
 
-    ws_r = last(4 * row_index, 4, 0)
-    ws_c = last(8 * col_index, 8, 32)
+    ws_r = last(4, 0, 0)
+    ws_c = last(8, 32, 4)
     blank = jnp.zeros((6, LANES), F32)
     copies = []
     for q in range(4):
@@ -439,20 +457,18 @@
     recv = exchange(send, "col")
     send, piece = call(first_kernel, [(32, 4, 4, LANES), (4, LANES)], held, recv)
     recv = exchange(send, "row")
-    qs, aq_rows, scals, previous = {}, {}, {}, None
+    qs, aq_rows, scals = {}, {}, {}
     for step in range(2, 9):
         args = [held, recv]
         if step in (2, 3):
             args.append(piece)
         if step > 2:
             args.append(scals[step - 2])
-        args += [qs[i] for i in range(1, step - 1)]
-        if step > 3:
-            args.append(previous)
+        args += [qs[i] for i in range(1, step - 1)] + [aq_rows[i] for i in range(1, step - 2)]
         groups = 4 if step in (2, 3) else 3
         outs = [(16 if step % 2 == 0 else 32, groups, 4, LANES), whole]
         if step > 2:
-            outs += [whole, (16, LANES)]
+            outs.append((16, LANES))
         outs.append((16, LANES))
         if step in (3, 4):
             outs.append((32 if step == 3 else 64, LANES))
@@ -462,7 +478,6 @@
         send = result.pop(0)
         qs[step - 1] = result.pop(0)
         if step > 2:
-            previous = result.pop(0)
             aq_rows[step - 2] = result.pop(0)
         scals[step - 1] = result.pop(0)
         if step == 3:
@@ -475,9 +490,9 @@
     (send,) = call(last_send_kernel, [(32, 1, 4, LANES)], recv)
     last = exchange(send, "row")
     rows, cols = matrix.shape
-    q, rest, reflect, side, left, right = call(
+    q, flag, reflect, side, left, right = call(
         panel_kernel,
-        [whole, whole, (8, rows), (104, LANES)]
+        [whole, jax.ShapeDtypeStruct((8, LANES), F32), (8, rows), (128, LANES)]
         + [VMEM((rows, LANES), jnp.bfloat16), VMEM((96, cols), jnp.bfloat16)],
         recv,
         packed,
@@ -486,19 +501,88 @@
         *[scals[i] for i in range(1, 8)],
         *[qs[i] for i in range(1, 8)],
         *[aq_rows[i] for i in range(1, 7)],
-        previous,
-        scratch=[whole, (16, LANES)],
+        scratch=[(16, LANES)],
         flops=40000000,
     )
     trailing = pl.pallas_call(
         trailing_kernel,
         out_shape=jax.ShapeDtypeStruct(matrix.shape, F32),
-        in_specs=[pl.BlockSpec(memory_space=VMEM)] * 7,
+        in_specs=[pl.BlockSpec(memory_space=VMEM)] * 6,
         out_specs=pl.BlockSpec(memory_space=pltpu.HBM),
-        scratch_shapes=[VMEM(whole, F32), VMEM(matrix.shape, F32), pltpu.SemaphoreType.DMA((4,))],
+        scratch_shapes=[VMEM(matrix.shape, F32), pltpu.SemaphoreType.DMA((4,))],
         compiler_params=pltpu.CompilerParams(vmem_limit_bytes=LIMIT),
-    )(held, last, q, rest, side, left, right)
+    )(held, last, q, side, left, right)
+    if not GUARD:
+        return trailing, reflect.T
+    kept = matrix
+    _, trailing, reflect = lax.while_loop(
+        lambda state: state[0] < 0.5,
+        lambda state: (jnp.float32(1.0), *column_by_column(kept)),
+        (flag[0, 0], trailing, reflect),
+    )
     return trailing, reflect.T
+
+
+def of_everyone(shard, axis):
+    size = lax.axis_size(axis)
+    return exchange(jnp.broadcast_to(shard[None], (size, *shard.shape)), axis)
+
+
+def column_by_column(matrix):
+    rows, cols = matrix.shape
+    row_at, col_at = lax.axis_index("row") * rows, lax.axis_index("col") * cols
+    panel = of_everyone(matrix[:, :COLS].T, "col")[0]
+    panel = of_everyone(panel, "row").transpose(1, 0, 2).reshape(COLS, N)
+    positions = jnp.arange(N, dtype=jnp.int32)
+
+    def one(column, state):
+        reflect, companion = state
+
+        def row(x):
+            return lax.dynamic_index_in_dim(x, column, 0, keepdims=False)
+
+        def entries(x):
+            return lax.dynamic_index_in_dim(x, column, 1, keepdims=True)
+
+        current = row(panel) - jnp.sum(
+            reflect * entries(companion) + companion * entries(reflect), axis=0
+        )
+        below = jnp.where(positions > column, current, 0.0)
+        leading = jnp.sum(jnp.where(positions == column + 1, current, 0.0))
+        length = jnp.sqrt(jnp.sum(below * below))
+        vector = below + jnp.where(positions == column + 1, length, 0.0)
+        scaling = 1.0 / (length * (length + leading))
+        along_rows_here = lax.dynamic_slice_in_dim(vector, row_at, rows, 0)
+        image = jnp.sum(matrix * along_rows_here[:, None], axis=0)
+        image = of_everyone(image, "row").sum(axis=0)
+        image = of_everyone(image, "col").reshape(N)
+        to_reflect = jnp.sum(companion * vector, axis=1, keepdims=True)
+        to_companion = jnp.sum(reflect * vector, axis=1, keepdims=True)
+        pushed = scaling * (
+            image - jnp.sum(reflect * to_reflect + companion * to_companion, axis=0)
+        )
+        update = pushed - 0.5 * scaling * jnp.sum(pushed * vector) * vector
+        reflect = lax.dynamic_update_index_in_dim(reflect, vector, column, 0)
+        return reflect, lax.dynamic_update_index_in_dim(companion, update, column, 0)
+
+    zero = jnp.zeros((COLS, N), F32)
+    reflect, companion = lax.fori_loop(0, COLS, one, (zero, zero))
+    reflect_rows = lax.dynamic_slice_in_dim(reflect, row_at, rows, 1)
+    companion_rows = lax.dynamic_slice_in_dim(companion, row_at, rows, 1)
+    reflect_cols = lax.dynamic_slice_in_dim(reflect, col_at, cols, 1)
+    companion_cols = lax.dynamic_slice_in_dim(companion, col_at, cols, 1)
+
+    def subtract(k, trailing):
+        def row(x):
+            return lax.dynamic_index_in_dim(x, k, 0, keepdims=False)
+
+        return (
+            trailing
+            - row(reflect_rows)[:, None] * row(companion_cols)[None, :]
+            - row(companion_rows)[:, None] * row(reflect_cols)[None, :]
+        )
+
+    return lax.fori_loop(0, COLS, subtract, matrix), reflect_rows
 
 
 def solution(mesh):

time: 159 us -> 158 us (level)
  transfers between devices with their start and end apart: 1 -> 1, of which waited for: 1 -> 1; matrix products, arithmetic and copies ran while one was open for 0% -> 0% of each run, Pallas kernels for 1% -> 2%
where the time goes in v4:
time: 158 us
  blocking collectives  136 us (86%)
  Pallas kernels  10.5 us (7%)
  waiting for transfers between devices  6.09 us (4%)
  starting transfers between devices  3.85 us (2%)
    all_to_all x9, blocking collectives, exchange(): return lax.all_to_all(x, axis, 0, 0, tiled=True)  136 us
    pallas_call x10, Pallas kernels, call(): pl.pallas_call(kernel, out_shape=[shape(x) for x in outs], in_specs=[pl.B...  6.9 us
    all_to_all x1, waiting for transfers between devices, exchange(): return lax.all_to_all(x, axis, 0, 0, tiled=True)  6.09 us
    all_to_all x1, starting transfers between devices, exchange(): return lax.all_to_all(x, axis, 0, 0, tiled=True)  3.85 us
  transfers between devices with their start and end apart: 1, of which 1 were waited for; matrix products, arithmetic and copies ran while one was open for 0% of the time, Pallas kernels for 2%

profile of v4, /device:TPU:1, one launch (start us, length us, event | category | flops | bytes accessed | tf_op | source)
XLA Modules:
  0.0 158.0 jit_solution(2181272243850577019)
XLA Ops:
  0.6 0.0 copy-start
  0.6 1.3 shard_map.30
  1.9 17.1 %all_to_all.50.recv_ref = f32[16,2,4,128]{3,2,1,0:T(4,128)S(1)} all-to-all(f32[16,2,4,128]{3,2,1,0:T(4,128)S(1)} %shard_map.30), channel_id=1, replica_groups=mesh['row'=32,'col'=16] {'col'}, dimensions={0} | all-to-all | bytes 131072 | tf_op jit(solution)/shard_map/all_to_all | solution.py:443
  19.0 0.0 copy-done
  19.0 0.3 shard_map.31
  19.3 23.6 %all_to_all.51.refs_1_ = f32[32,4,4,128]{3,2,1,0:T(4,128)S(1)} all-to-all(f32[32,4,4,128]{3,2,1,0:T(4,128)S(1)} %get-tuple-element.39), channel_id=1, replica_groups=mesh['row'=32,'col'=16] {'row'}, dimensions={0} | all-to-all | bytes 524288 | tf_op jit(solution)/shard_map/all_to_all | solution.py:443
  42.9 0.3 shard_map.32
  43.2 13.8 %all_to_all.52.refs_1_ = f32[16,4,4,128]{3,2,1,0:T(4,128)S(1)} all-to-all(f32[16,4,4,128]{3,2,1,0:T(4,128)S(1)} %get-tuple-element.41), channel_id=1, replica_groups=mesh['row'=32,'col'=16] {'col'}, dimensions={0} | all-to-all | bytes 262144 | tf_op jit(solution)/shard_map/all_to_all | solution.py:443
  57.0 0.5 shard_map.33
  57.5 15.6 %all_to_all.53.refs_1_ = f32[32,4,4,128]{3,2,1,0:T(4,128)S(1)} all-to-all(f32[32,4,4,128]{3,2,1,0:T(4,128)S(1)} %get-tuple-element.45), channel_id=1, replica_groups=mesh['row'=32,'col'=16] {'row'}, dimensions={0} | all-to-all | bytes 524288 | tf_op jit(solution)/shard_map/all_to_all | solution.py:443
  73.2 0.5 shard_map.34
  73.6 12.3 %all_to_all.54.refs_1_ = f32[16,3,4,128]{3,2,1,0:T(4,128)S(1)} all-to-all(f32[16,3,4,128]{3,2,1,0:T(4,128)S(1)} %get-tuple-element.49), channel_id=1, replica_groups=mesh['row'=32,'col'=16] {'col'}, dimensions={0} | all-to-all | bytes 196608 | tf_op jit(solution)/shard_map/all_to_all | solution.py:443
  86.0 0.5 shard_map.35
  86.5 14.1 %all_to_all.55.refs_1_ = f32[32,3,4,128]{3,2,1,0:T(4,128)S(1)} all-to-all(f32[32,3,4,128]{3,2,1,0:T(4,128)S(1)} %get-tuple-element.53), channel_id=1, replica_groups=mesh['row'=32,'col'=16] {'row'}, dimensions={0} | all-to-all | bytes 393216 | tf_op jit(solution)/shard_map/all_to_all | solution.py:443
  100.7 0.5 shard_map.36
  101.2 12.9 %all_to_all.56.refs_1_ = f32[16,3,4,128]{3,2,1,0:T(4,128)S(1)} all-to-all(f32[16,3,4,128]{3,2,1,0:T(4,128)S(1)} %get-tuple-element.57), channel_id=1, replica_groups=mesh['row'=32,'col'=16] {'col'}, dimensions={0} | all-to-all | bytes 196608 | tf_op jit(solution)/shard_map/all_to_all | solution.py:443
  114.1 0.6 shard_map.37
  114.7 13.8 %all_to_all.57.refs_1_ = f32[32,3,4,128]{3,2,1,0:T(4,128)S(1)} all-to-all(f32[32,3,4,128]{3,2,1,0:T(4,128)S(1)} %get-tuple-element.61), channel_id=1, replica_groups=mesh['row'=32,'col'=16] {'row'}, dimensions={0} | all-to-all | bytes 393216 | tf_op jit(solution)/shard_map/all_to_all | solution.py:443
  128.5 0.5 shard_map.38
  129.0 12.9 %all_to_all.58.recv_ref.refs_0_ = f32[16,3,4,128]{3,2,1,0:T(4,128)S(1)} all-to-all(f32[16,3,4,128]{3,2,1,0:T(4,128)S(1)} %get-tuple-element.65), channel_id=1, replica_groups=mesh['row'=32,'col'=16] {'col'}, dimensions={0} | all-to-all | bytes 196608 | tf_op jit(solution)/shard_map/all_to_all | solution.py:443
  141.9 0.7 shard_map.39
  142.6 3.9 %all-to-all-start.9 = ((f32[32,1,4,128]{3,2,1,0:T(4,128)}), f32[32,1,4,128]{3,2,1,0:T(4,128)S(1)}, u32[]{:S(2)}, u32[]{:S(2)}) async-start(f32[32,1,4,128]{3,2,1,0:T(4,128)} %shard_map.39), calls=%async_computation.9 | async-start | bytes 131072 | tf_op jit(solution)/shard_map/all_to_all | solution.py:443
  146.4 2.5 %shard_map.40 = (f32[128,128]{1,0:T(8,128)S(1)}, f32[8,128]{1,0:T(8,128)}, f32[8,512]{1,0:T(8,128)S(1)}, f32[128,128]{1,0:T(8,128)S(1)}, bf16[512,128]{1,0:T(8,128)(2,1)S(1)}, /*index=5*/bf16[96,1024]{1,0:T(8,128)(2,1)S(1)}) custom-call(f32[16,3,4,128]{3,2,1,0:T(4,128)S(1)} %all_to_all.58.recv_ref.refs_0_, f32[4,128]{1,0:T(4,128)S(1)} %get-tuple-element.42.refs_2_.refs_1_, ...), custom_call_target="tpu_custom_call" | custom-call | flops 40000000 | bytes 1000 | tf_op jit(solution)/shard_map/pallas_call | solution.py:431
  148.9 0.6 copy.3
  149.5 6.1 %all-to-all-done.9.recv_ref = f32[32,1,4,128]{3,2,1,0:T(4,128)S(1)} async-done(((f32[32,1,4,128]{3,2,1,0:T(4,128)}), f32[32,1,4,128]{3,2,1,0:T(4,128)S(1)}, u32[]{:S(2)}, u32[]{:S(2)}) %all-to-all-start.9) | async-done | bytes 65568 | tf_op jit(solution)/shard_map/all_to_all | solution.py:443
  155.6 2.4 %shard_map.41 = f32[512,1024]{1,0:T(8,128)} custom-call(f32[512,1024]{1,0:T(8,128)S(1)} %copy-done, f32[32,1,4,128]{3,2,1,0:T(4,128)S(1)} %all-to-all-done.9.recv_ref, f32[128,128]{1,0:T(8,128)S(1)} %get-tuple-element.71.q_ref, f32[128,128]{1,0:T(8,128)S(1)} %get-tuple-element.72.side_ref, bf16[512,128]{1,0:T(8,128)(2,1)S(1)} %get-tuple-element.73.left_ref, ...), custom_call_target="tpu_custom_call" | custom-call | tf_op jit(solution)/shard_map/pallas_call | solution.py:507
Async XLA Ops:
  0.6 18.3 %copy-start = (f32[512,1024]{1,0:T(8,128)S(1)}, f32[512,1024]{1,0:T(8,128)}, u32[]{:S(2)}) copy-start(f32[512,1024]{1,0:T(8,128)} %a_ref.5) | copy-start | bytes 6291460
  142.6 13.1 %all-to-all-start.9 = ((f32[32,1,4,128]{3,2,1,0:T(4,128)}), f32[32,1,4,128]{3,2,1,0:T(4,128)S(1)}, u32[]{:S(2)}, u32[]{:S(2)}) async-start(f32[32,1,4,128]{3,2,1,0:T(4,128)} %shard_map.39), calls=%async_computation.9 | async-start | bytes 131072 | tf_op jit(solution)/shard_map/all_to_all | solution.py:443

commit v5 on v4

--- a/solution.py
+++ b/solution.py
@@ -14,7 +14,7 @@
 F32 = jnp.float32
 VMEM = pltpu.VMEM
 LIMIT = 16 << 20
-GUARD = False
+GUARD = True
 GROWTH = 16.0
 PIVOT = 0.05
 
@@ -90,9 +90,11 @@
     )
 
 
-def start_kernel(a_ref, send_ref, slab_ref, sem):
-    copy = pltpu.make_async_copy(a_ref.at[:, pl.ds(0, LANES)], slab_ref, sem)
+def start_kernel(a_ref, send_ref, held_ref, slab_ref, sems):
+    copy = pltpu.make_async_copy(a_ref.at[:, pl.ds(0, LANES)], slab_ref, sems.at[0])
     copy.start()
+    hold = pltpu.make_async_copy(a_ref, held_ref, sems.at[1])
+    hold.start()
     copy.wait()
     left = [slab_ref[q * LANES : (q + 1) * LANES, :].T for q in range(4)]
     column = jnp.concatenate([x[0:1] for x in left], axis=0)
@@ -108,6 +110,7 @@
         rows = [left[2 * half + k][j + 1 : j + 2] for k in range(2)]
         send_ref[member, 0] = column
         send_ref[member, 1] = jnp.concatenate([*rows, packed, blank], axis=0)
+    hold.wait()
 
 
 def first_kernel(a_ref, recv_ref, send_ref, piece_ref):
@@ -445,15 +448,14 @@
 
 def local(matrix):
     whole = (N // LANES, LANES)
-    send = pl.pallas_call(
+    send, held = pl.pallas_call(
         start_kernel,
-        out_shape=VMEM((16, 2, 4, LANES), F32),
+        out_shape=[VMEM((16, 2, 4, LANES), F32), VMEM(matrix.shape, F32)],
         in_specs=[pl.BlockSpec(memory_space=pltpu.HBM)],
-        out_specs=pl.BlockSpec(memory_space=VMEM),
-        scratch_shapes=[VMEM((matrix.shape[0], LANES), F32), pltpu.SemaphoreType.DMA],
+        out_specs=[pl.BlockSpec(memory_space=VMEM)] * 2,
+        scratch_shapes=[VMEM((matrix.shape[0], LANES), F32), pltpu.SemaphoreType.DMA((2,))],
         compiler_params=pltpu.CompilerParams(vmem_limit_bytes=LIMIT),
     )(pltpu.with_memory_space_constraint(matrix, pltpu.HBM))
-    held = matrix
     recv = exchange(send, "col")
     send, piece = call(first_kernel, [(32, 4, 4, LANES), (4, LANES)], held, recv)
     recv = exchange(send, "row")
@@ -492,7 +494,7 @@
     rows, cols = matrix.shape
     q, flag, reflect, side, left, right = call(
         panel_kernel,
-        [whole, jax.ShapeDtypeStruct((8, LANES), F32), (8, rows), (128, LANES)]
+        [whole, jax.ShapeDtypeStruct((8, LANES), F32), pltpu.HBM((8, rows), F32), (128, LANES)]
         + [VMEM((rows, LANES), jnp.bfloat16), VMEM((96, cols), jnp.bfloat16)],
         recv,
         packed,
@@ -521,6 +523,10 @@
         (flag[0, 0], trailing, reflect),
     )
     return trailing, reflect.T
+
+
+def as_it_is(x_ref, out_ref):
+    out_ref[...] = x_ref[...]
 
 
 def of_everyone(shard, axis):
@@ -582,6 +588,7 @@
             - row(companion_rows)[:, None] * row(reflect_cols)[None, :]
         )
 
+    (reflect_rows,) = call(as_it_is, [(COLS, rows)], reflect_rows, pinned=False)
     return lax.fori_loop(0, COLS, subtract, matrix), reflect_rows
 
 

time: 158 us -> 160 us (1.013)
  no operation moved by 1% of the time
where the time goes in v5:
time: 160 us; the launch traced here: 159 us
  blocking collectives  136 us (85%)
  Pallas kernels  11 us (7%)
  waiting for transfers between devices  6.11 us (4%)
  starting transfers between devices  3.86 us (2%)
    all_to_all x9, blocking collectives, exchange(): return lax.all_to_all(x, axis, 0, 0, tiled=True)  136 us
    pallas_call x10, Pallas kernels, call(): pl.pallas_call(kernel, out_shape=[shape(x) for x in outs], in_specs=[pl.B...  6.93 us
    all_to_all x1, waiting for transfers between devices, exchange(): return lax.all_to_all(x, axis, 0, 0, tiled=True)  6.11 us
    all_to_all x1, starting transfers between devices, exchange(): return lax.all_to_all(x, axis, 0, 0, tiled=True)  3.86 us
  transfers between devices with their start and end apart: 1, of which 1 were waited for; matrix products, arithmetic and copies ran while one was open for 0% of the time, Pallas kernels for 2%

profile of v5, /device:TPU:1, one launch (start us, length us, event | category | flops | bytes accessed | tf_op | source)
XLA Modules:
  0.0 159.4 jit_solution(18118032003831324743)
XLA Ops:
  0.6 1.7 %shard_map.30 = (f32[16,2,4,128]{3,2,1,0:T(4,128)S(1)}, f32[512,1024]{1,0:T(8,128)S(1)}) custom-call(f32[512,1024]{1,0:T(8,128)} %a_ref.1), custom_call_target="tpu_custom_call" | custom-call | tf_op jit(solution)/shard_map/pallas_call | solution.py:451
  2.4 17.1 %all_to_all.93.recv_ref = f32[16,2,4,128]{3,2,1,0:T(4,128)S(1)} all-to-all(f32[16,2,4,128]{3,2,1,0:T(4,128)S(1)} %get-tuple-element.348), channel_id=1, replica_groups=mesh['row'=32,'col'=16] {'col'}, dimensions={0} | all-to-all | bytes 131072 | tf_op jit(solution)/shard_map/all_to_all | solution.py:446
  19.4 0.3 shard_map.31
  19.7 23.6 %all_to_all.94.refs_1_ = f32[32,4,4,128]{3,2,1,0:T(4,128)S(1)} all-to-all(f32[32,4,4,128]{3,2,1,0:T(4,128)S(1)} %get-tuple-element.349), channel_id=1, replica_groups=mesh['row'=32,'col'=16] {'row'}, dimensions={0} | all-to-all | bytes 524288 | tf_op jit(solution)/shard_map/all_to_all | solution.py:446
  43.3 0.3 shard_map.32
  43.7 13.8 %all_to_all.95.refs_1_ = f32[16,4,4,128]{3,2,1,0:T(4,128)S(1)} all-to-all(f32[16,4,4,128]{3,2,1,0:T(4,128)S(1)} %get-tuple-element.351), channel_id=1, replica_groups=mesh['row'=32,'col'=16] {'col'}, dimensions={0} | all-to-all | bytes 262144 | tf_op jit(solution)/shard_map/all_to_all | solution.py:446
  57.4 0.5 shard_map.33
  58.0 15.6 %all_to_all.96.refs_1_ = f32[32,4,4,128]{3,2,1,0:T(4,128)S(1)} all-to-all(f32[32,4,4,128]{3,2,1,0:T(4,128)S(1)} %get-tuple-element.355), channel_id=1, replica_groups=mesh['row'=32,'col'=16] {'row'}, dimensions={0} | all-to-all | bytes 524288 | tf_op jit(solution)/shard_map/all_to_all | solution.py:446
  73.6 0.5 shard_map.34
  74.1 12.3 %all_to_all.97.refs_1_ = f32[16,3,4,128]{3,2,1,0:T(4,128)S(1)} all-to-all(f32[16,3,4,128]{3,2,1,0:T(4,128)S(1)} %get-tuple-element.359), channel_id=1, replica_groups=mesh['row'=32,'col'=16] {'col'}, dimensions={0} | all-to-all | bytes 196608 | tf_op jit(solution)/shard_map/all_to_all | solution.py:446
  86.4 0.5 shard_map.35
  87.0 14.1 %all_to_all.98.refs_1_ = f32[32,3,4,128]{3,2,1,0:T(4,128)S(1)} all-to-all(f32[32,3,4,128]{3,2,1,0:T(4,128)S(1)} %get-tuple-element.363), channel_id=1, replica_groups=mesh['row'=32,'col'=16] {'row'}, dimensions={0} | all-to-all | bytes 393216 | tf_op jit(solution)/shard_map/all_to_all | solution.py:446
  101.1 0.5 shard_map.36
  101.6 12.9 %all_to_all.99.refs_1_ = f32[16,3,4,128]{3,2,1,0:T(4,128)S(1)} all-to-all(f32[16,3,4,128]{3,2,1,0:T(4,128)S(1)} %get-tuple-element.367), channel_id=1, replica_groups=mesh['row'=32,'col'=16] {'col'}, dimensions={0} | all-to-all | bytes 196608 | tf_op jit(solution)/shard_map/all_to_all | solution.py:446
  114.5 0.6 shard_map.37
  115.1 13.8 %all_to_all.100.refs_1_ = f32[32,3,4,128]{3,2,1,0:T(4,128)S(1)} all-to-all(f32[32,3,4,128]{3,2,1,0:T(4,128)S(1)} %get-tuple-element.371), channel_id=1, replica_groups=mesh['row'=32,'col'=16] {'row'}, dimensions={0} | all-to-all | bytes 393216 | tf_op jit(solution)/shard_map/all_to_all | solution.py:446
  128.9 0.5 shard_map.38
  129.4 12.9 %all_to_all.101.refs_0_.recv_ref = f32[16,3,4,128]{3,2,1,0:T(4,128)S(1)} all-to-all(f32[16,3,4,128]{3,2,1,0:T(4,128)S(1)} %get-tuple-element.375), channel_id=1, replica_groups=mesh['row'=32,'col'=16] {'col'}, dimensions={0} | all-to-all | bytes 196608 | tf_op jit(solution)/shard_map/all_to_all | solution.py:446
  142.4 0.7 shard_map.40
  143.0 3.9 %all-to-all-start.13 = ((f32[32,1,4,128]{3,2,1,0:T(4,128)}), f32[32,1,4,128]{3,2,1,0:T(4,128)S(1)}, u32[]{:S(2)}, u32[]{:S(2)}) async-start(f32[32,1,4,128]{3,2,1,0:T(4,128)} %shard_map.40), calls=%async_computation.13 | async-start | bytes 131072 | tf_op jit(solution)/shard_map/all_to_all | solution.py:446
  146.9 2.5 %shard_map.39 = (f32[128,128]{1,0:T(8,128)S(1)}, f32[8,128]{1,0:T(8,128)S(1)}, f32[8,512]{1,0:T(8,128)}, f32[128,128]{1,0:T(8,128)S(1)}, bf16[512,128]{1,0:T(8,128)(2,1)S(1)}, /*index=5*/bf16[96,1024]{1,0:T(8,128)(2,1)S(1)}) custom-call(f32[16,3,4,128]{3,2,1,0:T(4,128)S(1)} %all_to_all.101.refs_0_.recv_ref, f32[4,128]{1,0:T(4,128)S(1)} %get-tuple-element.352.refs_2_.refs_1_, ...), custom_call_target="tpu_custom_call" | custom-call | flops 40000000 | bytes 1000 | tf_op jit(solution)/shard_map/pallas_call | solution.py:434
  149.4 0.6 slice.9
  150.0 6.1 %all-to-all-done.13.recv_ref = f32[32,1,4,128]{3,2,1,0:T(4,128)S(1)} async-done(((f32[32,1,4,128]{3,2,1,0:T(4,128)}), f32[32,1,4,128]{3,2,1,0:T(4,128)S(1)}, u32[]{:S(2)}, u32[]{:S(2)}) %all-to-all-start.13) | async-done | bytes 65568 | tf_op jit(solution)/shard_map/all_to_all | solution.py:446
  156.1 2.4 %shard_map.41 = f32[512,1024]{1,0:T(8,128)} custom-call(f32[512,1024]{1,0:T(8,128)S(1)} %get-tuple-element.347.a_ref.refs_0_, f32[32,1,4,128]{3,2,1,0:T(4,128)S(1)} %all-to-all-done.13.recv_ref, f32[128,128]{1,0:T(8,128)S(1)} %get-tuple-element.382.q_ref, f32[128,128]{1,0:T(8,128)S(1)} %get-tuple-element.383.side_ref, ...), custom_call_target="tpu_custom_call" | custom-call | tf_op jit(solution)/shard_map/pallas_call | solution.py:509
  158.5 0.8 while.39
Async XLA Ops:
  143.0 13.1 %all-to-all-start.13 = ((f32[32,1,4,128]{3,2,1,0:T(4,128)}), f32[32,1,4,128]{3,2,1,0:T(4,128)S(1)}, u32[]{:S(2)}, u32[]{:S(2)}) async-start(f32[32,1,4,128]{3,2,1,0:T(4,128)} %shard_map.40), calls=%async_computation.13 | async-start | bytes 131072 | tf_op jit(solution)/shard_map/all_to_all | solution.py:446

commit v6 on v5

--- a/solution.py
+++ b/solution.py
@@ -407,20 +407,24 @@
     blank = jnp.zeros((6, LANES), F32)
     copies = []
     for q in range(4):
-        at = slice(q * LANES, (q + 1) * LANES)
         upright = jnp.concatenate([side_ref[8 * q + 7 : 8 * q + 8, :], ws_r[q], blank], axis=0).T
-        change = jnp.dot(left_ref[at, 0:96], right_ref[...], preferred_element_type=F32)
-        for t in range(8):
-            to = slice(t * LANES, (t + 1) * LANES)
-            block_ref[at, to] = (
-                a_ref[at, to]
-                - change[:, to]
-                - upright[:, 0:1] * ws_c[t]
-                - upright[:, 1:2] * side_ref[39 + 8 * t : 40 + 8 * t, :]
+        for half in range(2):
+            at = slice(q * LANES + half * 64, q * LANES + half * 64 + 64)
+            piece = upright[half * 64 : half * 64 + 64]
+            change = jnp.dot(left_ref[at, 0:96], right_ref[...], preferred_element_type=F32)
+            for t in range(8):
+                to = slice(t * LANES, (t + 1) * LANES)
+                block_ref[at, to] = (
+                    a_ref[at, to]
+                    - change[:, to]
+                    - piece[:, 0:1] * ws_c[t]
+                    - piece[:, 1:2] * side_ref[39 + 8 * t : 40 + 8 * t, :]
+                )
+            copy = pltpu.make_async_copy(
+                block_ref.at[at, :], out_ref.at[at, :], sems.at[2 * q + half]
             )
-        copy = pltpu.make_async_copy(block_ref.at[at, :], out_ref.at[at, :], sems.at[q])
-        copy.start()
-        copies.append(copy)
+            copy.start()
+            copies.append(copy)
     for copy in copies:
         copy.wait()
 
@@ -511,16 +515,15 @@
         out_shape=jax.ShapeDtypeStruct(matrix.shape, F32),
         in_specs=[pl.BlockSpec(memory_space=VMEM)] * 6,
         out_specs=pl.BlockSpec(memory_space=pltpu.HBM),
-        scratch_shapes=[VMEM(matrix.shape, F32), pltpu.SemaphoreType.DMA((4,))],
+        scratch_shapes=[VMEM(matrix.shape, F32), pltpu.SemaphoreType.DMA((8,))],
         compiler_params=pltpu.CompilerParams(vmem_limit_bytes=LIMIT),
     )(held, last, q, side, left, right)
     if not GUARD:
         return trailing, reflect.T
-    kept = matrix
     _, trailing, reflect = lax.while_loop(
-        lambda state: state[0] < 0.5,
-        lambda state: (jnp.float32(1.0), *column_by_column(kept)),
-        (flag[0, 0], trailing, reflect),
+        lambda state: state[0],
+        lambda state: (jnp.bool_(False), *column_by_column(matrix)),
+        (flag[0, 0] < 0.5, trailing, reflect),
     )
     return trailing, reflect.T
 

time: 160 us -> 159 us (level)
  no operation moved by 1% of the time
where the time goes in v6:
time: 159 us
  blocking collectives  136 us (86%)
  Pallas kernels  11 us (7%)
  waiting for transfers between devices  5.46 us (3%)
  starting transfers between devices  3.86 us (2%)
    all_to_all x9, blocking collectives, exchange(): return lax.all_to_all(x, axis, 0, 0, tiled=True)  136 us
    pallas_call x10, Pallas kernels, call(): pl.pallas_call(kernel, out_shape=[shape(x) for x in outs], in_specs=[pl.B...  6.93 us
    all_to_all x1, waiting for transfers between devices, exchange(): return lax.all_to_all(x, axis, 0, 0, tiled=True)  5.46 us
    all_to_all x1, starting transfers between devices, exchange(): return lax.all_to_all(x, axis, 0, 0, tiled=True)  3.86 us
  transfers between devices with their start and end apart: 1, of which 1 were waited for; matrix products, arithmetic and copies ran while one was open for 0% of the time, Pallas kernels for 2%

profile of v6, /device:TPU:1, one launch (start us, length us, event | category | flops | bytes accessed | tf_op | source)
XLA Modules:
  0.0 158.8 jit_solution(5241798452006492039)
XLA Ops:
  0.6 1.7 %shard_map.30 = (f32[16,2,4,128]{3,2,1,0:T(4,128)S(1)}, f32[512,1024]{1,0:T(8,128)S(1)}) custom-call(f32[512,1024]{1,0:T(8,128)} %a_ref.1), custom_call_target="tpu_custom_call" | custom-call | tf_op jit(solution)/shard_map/pallas_call | solution.py:455
  2.4 17.1 %all_to_all.93.recv_ref = f32[16,2,4,128]{3,2,1,0:T(4,128)S(1)} all-to-all(f32[16,2,4,128]{3,2,1,0:T(4,128)S(1)} %get-tuple-element.348), channel_id=1, replica_groups=mesh['row'=32,'col'=16] {'col'}, dimensions={0} | all-to-all | bytes 131072 | tf_op jit(solution)/shard_map/all_to_all | solution.py:450
  19.4 0.3 shard_map.31
  19.7 23.6 %all_to_all.94.refs_1_ = f32[32,4,4,128]{3,2,1,0:T(4,128)S(1)} all-to-all(f32[32,4,4,128]{3,2,1,0:T(4,128)S(1)} %get-tuple-element.349), channel_id=1, replica_groups=mesh['row'=32,'col'=16] {'row'}, dimensions={0} | all-to-all | bytes 524288 | tf_op jit(solution)/shard_map/all_to_all | solution.py:450
  43.3 0.3 shard_map.32
  43.7 13.8 %all_to_all.95.refs_1_ = f32[16,4,4,128]{3,2,1,0:T(4,128)S(1)} all-to-all(f32[16,4,4,128]{3,2,1,0:T(4,128)S(1)} %get-tuple-element.351), channel_id=1, replica_groups=mesh['row'=32,'col'=16] {'col'}, dimensions={0} | all-to-all | bytes 262144 | tf_op jit(solution)/shard_map/all_to_all | solution.py:450
  57.4 0.5 shard_map.33
  58.0 15.6 %all_to_all.96.refs_1_ = f32[32,4,4,128]{3,2,1,0:T(4,128)S(1)} all-to-all(f32[32,4,4,128]{3,2,1,0:T(4,128)S(1)} %get-tuple-element.355), channel_id=1, replica_groups=mesh['row'=32,'col'=16] {'row'}, dimensions={0} | all-to-all | bytes 524288 | tf_op jit(solution)/shard_map/all_to_all | solution.py:450
  73.6 0.5 shard_map.34
  74.1 12.3 %all_to_all.97.refs_1_ = f32[16,3,4,128]{3,2,1,0:T(4,128)S(1)} all-to-all(f32[16,3,4,128]{3,2,1,0:T(4,128)S(1)} %get-tuple-element.359), channel_id=1, replica_groups=mesh['row'=32,'col'=16] {'col'}, dimensions={0} | all-to-all | bytes 196608 | tf_op jit(solution)/shard_map/all_to_all | solution.py:450
  86.4 0.5 shard_map.35
  87.0 14.1 %all_to_all.98.refs_1_ = f32[32,3,4,128]{3,2,1,0:T(4,128)S(1)} all-to-all(f32[32,3,4,128]{3,2,1,0:T(4,128)S(1)} %get-tuple-element.363), channel_id=1, replica_groups=mesh['row'=32,'col'=16] {'row'}, dimensions={0} | all-to-all | bytes 393216 | tf_op jit(solution)/shard_map/all_to_all | solution.py:450
  101.1 0.5 shard_map.36
  101.6 12.9 %all_to_all.99.refs_1_ = f32[16,3,4,128]{3,2,1,0:T(4,128)S(1)} all-to-all(f32[16,3,4,128]{3,2,1,0:T(4,128)S(1)} %get-tuple-element.367), channel_id=1, replica_groups=mesh['row'=32,'col'=16] {'col'}, dimensions={0} | all-to-all | bytes 196608 | tf_op jit(solution)/shard_map/all_to_all | solution.py:450
  114.5 0.6 shard_map.37
  115.1 13.8 %all_to_all.100.refs_1_ = f32[32,3,4,128]{3,2,1,0:T(4,128)S(1)} all-to-all(f32[32,3,4,128]{3,2,1,0:T(4,128)S(1)} %get-tuple-element.371), channel_id=1, replica_groups=mesh['row'=32,'col'=16] {'row'}, dimensions={0} | all-to-all | bytes 393216 | tf_op jit(solution)/shard_map/all_to_all | solution.py:450
  128.9 0.5 shard_map.38
  129.4 12.9 %all_to_all.101.refs_0_.recv_ref = f32[16,3,4,128]{3,2,1,0:T(4,128)S(1)} all-to-all(f32[16,3,4,128]{3,2,1,0:T(4,128)S(1)} %get-tuple-element.375), channel_id=1, replica_groups=mesh['row'=32,'col'=16] {'col'}, dimensions={0} | all-to-all | bytes 196608 | tf_op jit(solution)/shard_map/all_to_all | solution.py:450
  142.4 0.7 shard_map.40
  143.0 3.9 %all-to-all-start.13 = ((f32[32,1,4,128]{3,2,1,0:T(4,128)}), f32[32,1,4,128]{3,2,1,0:T(4,128)S(1)}, u32[]{:S(2)}, u32[]{:S(2)}) async-start(f32[32,1,4,128]{3,2,1,0:T(4,128)} %shard_map.40), calls=%async_computation.13 | async-start | bytes 131072 | tf_op jit(solution)/shard_map/all_to_all | solution.py:450
  146.9 2.5 %shard_map.39 = (f32[128,128]{1,0:T(8,128)S(1)}, f32[8,128]{1,0:T(8,128)S(1)}, f32[8,512]{1,0:T(8,128)}, f32[128,128]{1,0:T(8,128)S(1)}, bf16[512,128]{1,0:T(8,128)(2,1)S(1)}, /*index=5*/bf16[96,1024]{1,0:T(8,128)(2,1)S(1)}) custom-call(f32[16,3,4,128]{3,2,1,0:T(4,128)S(1)} %all_to_all.101.refs_0_.recv_ref, f32[4,128]{1,0:T(4,128)S(1)} %get-tuple-element.352.refs_2_.refs_1_, ...), custom_call_target="tpu_custom_call" | custom-call | flops 40000000 | bytes 1000 | tf_op jit(solution)/shard_map/pallas_call | solution.py:438
  149.4 0.6 slice.9
  150.6 5.5 %all-to-all-done.13.recv_ref = f32[32,1,4,128]{3,2,1,0:T(4,128)S(1)} async-done(((f32[32,1,4,128]{3,2,1,0:T(4,128)}), f32[32,1,4,128]{3,2,1,0:T(4,128)S(1)}, u32[]{:S(2)}, u32[]{:S(2)}) %all-to-all-start.13) | async-done | bytes 65568 | tf_op jit(solution)/shard_map/all_to_all | solution.py:450
  156.1 2.3 %shard_map.41 = f32[512,1024]{1,0:T(8,128)} custom-call(f32[512,1024]{1,0:T(8,128)S(1)} %get-tuple-element.347.a_ref.refs_0_, f32[32,1,4,128]{3,2,1,0:T(4,128)S(1)} %all-to-all-done.13.recv_ref, f32[128,128]{1,0:T(8,128)S(1)} %get-tuple-element.382.q_ref, f32[128,128]{1,0:T(8,128)S(1)} %get-tuple-element.383.side_ref, ...), custom_call_target="tpu_custom_call" | custom-call | tf_op jit(solution)/shard_map/pallas_call | solution.py:513
  158.4 0.2 while.39
Async XLA Ops:
  143.0 13.1 %all-to-all-start.13 = ((f32[32,1,4,128]{3,2,1,0:T(4,128)}), f32[32,1,4,128]{3,2,1,0:T(4,128)S(1)}, u32[]{:S(2)}, u32[]{:S(2)}) async-start(f32[32,1,4,128]{3,2,1,0:T(4,128)} %shard_map.40), calls=%async_computation.13 | async-start | bytes 131072 | tf_op jit(solution)/shard_map/all_to_all | solution.py:450

commit v7 on v6

--- a/solution.py
+++ b/solution.py
@@ -137,25 +137,28 @@
 def settle(step, given, scal, qs):
     u = without_first(given, None) if step == 2 else given
     zero = jnp.zeros((1, LANES), F32)
-    w, cs, growth = u, {}, zero + 1.0
+    w, cs, growth = u, {}, 0.0
+    known = range(1, step - 1)
+    rows = [jnp.sum(u * qs[i], axis=0, keepdims=True) for i in known]
+    rows = rows + [zero] * (7 - len(rows)) + [jnp.sum(u * u, axis=0, keepdims=True)]
+    sums = jnp.sum(jnp.concatenate(rows, axis=0), axis=1, keepdims=True)
+    squared = sums[7:8, 0:1]
     if step == 2:
         alpha = shift = given[0:1, 0:1]
     else:
-        known = range(1, step - 1)
-        rows = [jnp.sum(u * qs[i], axis=0, keepdims=True) for i in known]
-        rows = rows + [zero] * (8 - len(rows))
-        sums = jnp.sum(jnp.concatenate(rows, axis=0), axis=1, keepdims=True)
         for i in known:
             cs[i] = sums[i - 1 : i, 0:1]
             w = w - cs[i] * qs[i]
-        growth = jnp.sum(sums * sums, axis=0, keepdims=True)
+        growth = jnp.sum(jnp.where(iota((8, 1), 0) < 7, sums * sums, 0.0), axis=0, keepdims=True)
+        squared = squared - growth
         alpha, before = cs[step - 2] + coefficient(scal, 9), coefficient(scal, 10)
         smaller = jnp.where(jnp.abs(alpha) < jnp.abs(before), alpha, before)
         shift = jnp.where(alpha * before > 0.0, smaller, 0.0)
-    length = jnp.sqrt(total(w * w))
+    length = jnp.sqrt(squared)
     inverse = 1.0 / length
+    growth = 1.0 + growth * inverse * inverse
     if step > 2:
-        growth = coefficient(scal, 11) * (1.0 + growth * inverse * inverse)
+        growth = growth * coefficient(scal, 11)
     out = [zero + length] + [zero + cs[i] if i in cs else zero for i in range(1, 8)]
     out = out + [zero + x for x in (inverse, shift, alpha, growth)] + [zero] * 4
     return w * inverse, length, inverse, shift, cs, jnp.concatenate(out, axis=0)
@@ -164,7 +167,7 @@
 def given_rows(recv_ref, by_rows):
     row_index, col_index = places()
     if by_rows:
-        group = recv_ref.shape[1] - 1 if recv_ref.shape[1] < 3 else 2
+        group = 2 if recv_ref.shape[1] > 2 else 0
         here = recv_ref[row_index, group]
         there = [recv_ref[2 * col_index + k, group] for k in range(2)]
         first = recv_ref[0, group][0:1]
@@ -197,7 +200,7 @@
     a_ref, recv_ref = refs[:2]
     del refs[:2]
     row_index, col_index = places()
-    piece_ref = refs.pop(0) if step in (2, 3) else None
+    piece_ref = refs.pop(0) if step == 2 else None
     scal = refs.pop(0)[...] if step > 2 else None
     q_refs = {i: refs.pop(0) for i in range(1, step - 1)}
     rows_refs = {i: refs.pop(0) for i in range(1, step - 2)}
@@ -206,7 +209,7 @@
     if step > 2:
         rows_refs[step - 2] = refs.pop(0)
     scal_ref = refs.pop(0)
-    edge_ref = refs.pop(0) if step in (3, 4) else None
+    edge_ref = refs.pop(0) if step == 3 else None
     new_piece_ref = refs.pop(0) if step == 2 else None
 
     even = step % 2 == 0
@@ -227,7 +230,10 @@
     here = y_here
     for i in cs:
         here = here - cs[i] * rows_refs[i][part, :]
-    here = here * inverse - shift * q_ref[at, :]
+    q_here = without_first(given_rows(recv_ref, even)[part], chunk)
+    for i in cs:
+        q_here = q_here - cs[i] * q_refs[i][at, :]
+    here = (here - shift * q_here) * inverse
     if step > 2:
         here = here - length * q_refs[step - 2][at, :]
     here = without_first(here, chunk)
@@ -237,18 +243,16 @@
     else:
         send_all(send_ref, 0, halves(times_rows(a_ref, here)))
         send_all(send_ref, 2, [here])
-    if step in (2, 3):
+    if step == 2:
         send_all(send_ref, 3, [piece_ref[...]])
     if step == 2:
         new_piece_ref[...] = recv_ref[0, 3]
     if step == 3:
         edge_ref[...] = jnp.concatenate([recv_ref[c, 3][0:2] for c in range(16)], axis=0)
-    if step == 4:
-        edge_ref[...] = jnp.concatenate([recv_ref[r, 3][0:2] for r in range(32)], axis=0)
-
-
-def last_send_kernel(recv_ref, send_ref):
-    send_all(send_ref, 0, [along_rows(recv_ref)])
+
+
+def last_send_kernel(recv_ref, piece_ref, send_ref):
+    send_all(send_ref, 0, [along_rows(recv_ref), piece_ref[...]])
 
 
 def sign(k):
@@ -289,11 +293,11 @@
     row_index, col_index = places()
     refs = list(refs)
     refs.insert(0, None)
-    recv_ref, packed_ref, edge_r_ref, edge_c_ref = refs[1:5]
-    scal_refs = {i: refs[4 + i] for i in range(1, 8)}
-    q_refs = {i: refs[11 + i] for i in range(1, 8)}
-    aq_rows = {i: refs[18 + i] for i in range(1, 7)}
-    q_out, flag_ref, reflect_ref, side_ref, left_ref, right_ref, rows_out = refs[25:32]
+    recv_ref, packed_ref, edge_r_ref = refs[1:4]
+    scal_refs = {i: refs[3 + i] for i in range(1, 8)}
+    q_refs = {i: refs[10 + i] for i in range(1, 8)}
+    aq_rows = {i: refs[17 + i] for i in range(1, 7)}
+    q_out, flag_ref, reflect_ref, side_ref, left_ref, right_ref, rows_out = refs[24:31]
     q, length, _, _, cs, scal = settle(
         9, whole_from_cols(recv_ref, 1), scal_refs[7][...], {i: r[...] for i, r in q_refs.items()}
     )
@@ -355,10 +359,11 @@
         for t in range(count):
             row = base + t
             d = d_tile(q_refs, row)
-            edge = jnp.concatenate(
-                [edge_ref[count * k + t : count * k + t + 1, :] for k in range(8)], axis=0
-            )
-            ad = edge - rows_at(aq_rows, kept + t)
+            ad = -rows_at(aq_rows, kept + t)
+            if edge_ref is not None:
+                ad = ad + jnp.concatenate(
+                    [edge_ref[count * k + t : count * k + t + 1, :] for k in range(8)], axis=0
+                )
             ds.append(d)
             ys.append(product(factor, ad) - 0.5 * product(core, d))
             side_ref[first + 8 * t : first + 8 * t + 8, :] = product(flipped, d)
@@ -369,13 +374,16 @@
         high, middle, low = three(jnp.concatenate([ds[t], ys[t]], axis=0))
         stack = [high, high, middle, middle, high, low, jnp.zeros((32, LANES), F32)]
         at = slice(t * LANES, (t + 1) * LANES)
-        left_ref[at, :] = jnp.concatenate(stack, axis=0).T.astype(jnp.bfloat16)
+        left_ref[at, 0:LANES] = jnp.concatenate(stack, axis=0).T.astype(jnp.bfloat16)
+        high, middle, low = three(side_ref[8 * t : 8 * t + 8, :])
+        stack = [high, high, middle, middle, high, low, jnp.zeros((80, LANES), F32)]
+        left_ref[at, LANES:] = jnp.concatenate(stack, axis=0).T.astype(jnp.bfloat16)
         out = jnp.zeros((8, LANES), F32)
         for k in range(8):
             out = out + to_reflect[:, k : k + 1] * ds[t][k : k + 1, :]
         out = jnp.where((4 * row_index + t == 0) & (lanes <= ks), 0.0, out)
         reflect_ref[:, t * LANES : (t + 1) * LANES] = out
-    ds, ys = tiles(8 * col_index, 8, edge_c_ref, 32, 4)
+    ds, ys = tiles(8 * col_index, 8, None, 32, 4)
     for t in range(8):
         high, middle, low = three(jnp.concatenate([ys[t], ds[t]], axis=0))
         stack = [high, middle, high, middle, low, high]
@@ -384,8 +392,15 @@
 
 
 def trailing_kernel(
-    a_ref, recv_ref, q_ref, side_ref, left_ref, right_ref, out_ref, block_ref, sems
+    a_ref, recv_ref, q_ref, side_ref, left_ref, right_ref, out_ref, block_ref, edge_ref, sems
 ):
+    for t in range(8):
+        members = [divmod(8 * k + t, 2) for k in range(8)]
+        high, middle, low = three(
+            jnp.concatenate([recv_ref[r, 1][i : i + 1] for r, i in members], axis=0)
+        )
+        stack = jnp.concatenate([high, middle, high, middle, low, high], axis=0)
+        edge_ref[:, t * LANES : (t + 1) * LANES] = stack.astype(jnp.bfloat16)
     inverse = coefficient(side_ref, 96)
     aq = (given_rows(recv_ref, True) - side_ref[104:120, :]) * inverse
     alpha = total(q_ref[...] * whole_from_rows(recv_ref, 0)) - coefficient(side_ref, 120)
@@ -412,6 +427,8 @@
             at = slice(q * LANES + half * 64, q * LANES + half * 64 + 64)
             piece = upright[half * 64 : half * 64 + 64]
             change = jnp.dot(left_ref[at, 0:96], right_ref[...], preferred_element_type=F32)
+            edge = left_ref[at, LANES : LANES + 48]
+            change = change + jnp.dot(edge, edge_ref[...], preferred_element_type=F32)
             for t in range(8):
                 to = slice(t * LANES, (t + 1) * LANES)
                 block_ref[at, to] = (
@@ -466,18 +483,18 @@
     qs, aq_rows, scals = {}, {}, {}
     for step in range(2, 9):
         args = [held, recv]
-        if step in (2, 3):
+        if step == 2:
             args.append(piece)
         if step > 2:
             args.append(scals[step - 2])
         args += [qs[i] for i in range(1, step - 1)] + [aq_rows[i] for i in range(1, step - 2)]
-        groups = 4 if step in (2, 3) else 3
+        groups = 4 if step == 2 else 3
         outs = [(16 if step % 2 == 0 else 32, groups, 4, LANES), whole]
         if step > 2:
             outs.append((16, LANES))
         outs.append((16, LANES))
-        if step in (3, 4):
-            outs.append((32 if step == 3 else 64, LANES))
+        if step == 3:
+            outs.append((32, LANES))
         if step == 2:
             outs.append((4, LANES))
         result = list(call(functools.partial(step_kernel, step), outs, *args))
@@ -488,22 +505,19 @@
         scals[step - 1] = result.pop(0)
         if step == 3:
             edge_r = result.pop(0)
-        if step == 4:
-            edge_c = result.pop(0)
         if step == 2:
             piece = packed = result.pop(0)
         recv = exchange(send, "col" if step % 2 == 0 else "row")
-    (send,) = call(last_send_kernel, [(32, 1, 4, LANES)], recv)
+    (send,) = call(last_send_kernel, [(32, 2, 4, LANES)], recv, packed)
     last = exchange(send, "row")
     rows, cols = matrix.shape
     q, flag, reflect, side, left, right = call(
         panel_kernel,
         [whole, jax.ShapeDtypeStruct((8, LANES), F32), pltpu.HBM((8, rows), F32), (128, LANES)]
-        + [VMEM((rows, LANES), jnp.bfloat16), VMEM((96, cols), jnp.bfloat16)],
+        + [VMEM((rows, 2 * LANES), jnp.bfloat16), VMEM((96, cols), jnp.bfloat16)],
         recv,
         packed,
         edge_r,
-        edge_c,
         *[scals[i] for i in range(1, 8)],
         *[qs[i] for i in range(1, 8)],
         *[aq_rows[i] for i in range(1, 7)],
@@ -515,7 +529,11 @@
         out_shape=jax.ShapeDtypeStruct(matrix.shape, F32),
         in_specs=[pl.BlockSpec(memory_space=VMEM)] * 6,
         out_specs=pl.BlockSpec(memory_space=pltpu.HBM),
-        scratch_shapes=[VMEM(matrix.shape, F32), pltpu.SemaphoreType.DMA((8,))],
+        scratch_shapes=[
+            VMEM(matrix.shape, F32),
+            VMEM((48, cols), jnp.bfloat16),
+            pltpu.SemaphoreType.DMA((8,)),
+        ],
         compiler_params=pltpu.CompilerParams(vmem_limit_bytes=LIMIT),
     )(held, last, q, side, left, right)
     if not GUARD:

time: 159 us -> 158 us (level)
  transfers between devices with their start and end apart: 1 -> 1, of which waited for: 1 -> 1; matrix products, arithmetic and copies ran while one was open for 0% -> 0% of each run, Pallas kernels for 2% -> 1%
where the time goes in v7:
time: 158 us
  blocking collectives  135 us (85%)
  Pallas kernels  10 us (6%)
  waiting for transfers between devices  6.67 us (4%)
  starting transfers between devices  3.86 us (2%)
    all_to_all x9, blocking collectives, exchange(): return lax.all_to_all(x, axis, 0, 0, tiled=True)  135 us
    all_to_all x1, waiting for transfers between devices, exchange(): return lax.all_to_all(x, axis, 0, 0, tiled=True)  6.67 us
    pallas_call x10, Pallas kernels, call(): pl.pallas_call(kernel, out_shape=[shape(x) for x in outs], in_specs=[pl.B...  5.98 us
    all_to_all x1, starting transfers between devices, exchange(): return lax.all_to_all(x, axis, 0, 0, tiled=True)  3.86 us
  transfers between devices with their start and end apart: 1, of which 1 were waited for; matrix products, arithmetic and copies ran while one was open for 0% of the time, Pallas kernels for 1%

profile of v7, /device:TPU:1, one launch (start us, length us, event | category | flops | bytes accessed | tf_op | source)
XLA Modules:
  0.0 157.5 jit_solution(16011263234585362017)
XLA Ops:
  0.6 1.7 %shard_map.30 = (f32[16,2,4,128]{3,2,1,0:T(4,128)S(1)}, f32[512,1024]{1,0:T(8,128)S(1)}) custom-call(f32[512,1024]{1,0:T(8,128)} %a_ref.1), custom_call_target="tpu_custom_call" | custom-call | tf_op jit(solution)/shard_map/pallas_call | solution.py:472
  2.4 17.1 %all_to_all.93.recv_ref = f32[16,2,4,128]{3,2,1,0:T(4,128)S(1)} all-to-all(f32[16,2,4,128]{3,2,1,0:T(4,128)S(1)} %get-tuple-element.347), channel_id=1, replica_groups=mesh['row'=32,'col'=16] {'col'}, dimensions={0} | all-to-all | bytes 131072 | tf_op jit(solution)/shard_map/all_to_all | solution.py:467
  19.4 0.3 shard_map.31
  19.7 23.6 %all_to_all.94.refs_1_ = f32[32,4,4,128]{3,2,1,0:T(4,128)S(1)} all-to-all(f32[32,4,4,128]{3,2,1,0:T(4,128)S(1)} %get-tuple-element.348), channel_id=1, replica_groups=mesh['row'=32,'col'=16] {'row'}, dimensions={0} | all-to-all | bytes 524288 | tf_op jit(solution)/shard_map/all_to_all | solution.py:467
  43.3 0.3 shard_map.32
  43.7 13.8 %all_to_all.95.refs_1_ = f32[16,4,4,128]{3,2,1,0:T(4,128)S(1)} all-to-all(f32[16,4,4,128]{3,2,1,0:T(4,128)S(1)} %get-tuple-element.350), channel_id=1, replica_groups=mesh['row'=32,'col'=16] {'col'}, dimensions={0} | all-to-all | bytes 262144 | tf_op jit(solution)/shard_map/all_to_all | solution.py:467
  57.4 0.5 shard_map.33
  57.9 14.3 %all_to_all.96.refs_1_ = f32[32,3,4,128]{3,2,1,0:T(4,128)S(1)} all-to-all(f32[32,3,4,128]{3,2,1,0:T(4,128)S(1)} %get-tuple-element.353), channel_id=1, replica_groups=mesh['row'=32,'col'=16] {'row'}, dimensions={0} | all-to-all | bytes 393216 | tf_op jit(solution)/shard_map/all_to_all | solution.py:467
  72.3 0.4 shard_map.34
  72.6 12.5 %all_to_all.97.refs_1_ = f32[16,3,4,128]{3,2,1,0:T(4,128)S(1)} all-to-all(f32[16,3,4,128]{3,2,1,0:T(4,128)S(1)} %get-tuple-element.357), channel_id=1, replica_groups=mesh['row'=32,'col'=16] {'col'}, dimensions={0} | all-to-all | bytes 196608 | tf_op jit(solution)/shard_map/all_to_all | solution.py:467
  85.2 0.5 shard_map.35
  85.6 13.8 %all_to_all.98.refs_1_ = f32[32,3,4,128]{3,2,1,0:T(4,128)S(1)} all-to-all(f32[32,3,4,128]{3,2,1,0:T(4,128)S(1)} %get-tuple-element.361), channel_id=1, replica_groups=mesh['row'=32,'col'=16] {'row'}, dimensions={0} | all-to-all | bytes 393216 | tf_op jit(solution)/shard_map/all_to_all | solution.py:467
  99.5 0.4 shard_map.36
  99.8 12.9 %all_to_all.99.refs_1_ = f32[16,3,4,128]{3,2,1,0:T(4,128)S(1)} all-to-all(f32[16,3,4,128]{3,2,1,0:T(4,128)S(1)} %get-tuple-element.365), channel_id=1, replica_groups=mesh['row'=32,'col'=16] {'col'}, dimensions={0} | all-to-all | bytes 196608 | tf_op jit(solution)/shard_map/all_to_all | solution.py:467
  112.8 0.5 shard_map.37
  113.3 13.8 %all_to_all.100.refs_1_ = f32[32,3,4,128]{3,2,1,0:T(4,128)S(1)} all-to-all(f32[32,3,4,128]{3,2,1,0:T(4,128)S(1)} %get-tuple-element.369), channel_id=1, replica_groups=mesh['row'=32,'col'=16] {'row'}, dimensions={0} | all-to-all | bytes 393216 | tf_op jit(solution)/shard_map/all_to_all | solution.py:467
  127.1 0.4 shard_map.38
  127.5 12.9 %all_to_all.101.refs_0_.recv_ref = f32[16,3,4,128]{3,2,1,0:T(4,128)S(1)} all-to-all(f32[16,3,4,128]{3,2,1,0:T(4,128)S(1)} %get-tuple-element.373), channel_id=1, replica_groups=mesh['row'=32,'col'=16] {'col'}, dimensions={0} | all-to-all | bytes 196608 | tf_op jit(solution)/shard_map/all_to_all | solution.py:467
  140.4 0.7 shard_map.40
  141.1 3.9 %all-to-all-start.13 = ((f32[32,2,4,128]{3,2,1,0:T(4,128)}), f32[32,2,4,128]{3,2,1,0:T(4,128)S(1)}, u32[]{:S(2)}, u32[]{:S(2)}) async-start(f32[32,2,4,128]{3,2,1,0:T(4,128)} %shard_map.40), calls=%async_computation.13 | async-start | bytes 262144 | tf_op jit(solution)/shard_map/all_to_all | solution.py:467
  145.0 2.1 %shard_map.39 = (f32[128,128]{1,0:T(8,128)S(1)}, f32[8,128]{1,0:T(8,128)S(1)}, f32[8,512]{1,0:T(8,128)}, f32[128,128]{1,0:T(8,128)S(1)}, bf16[512,256]{1,0:T(8,128)(2,1)S(1)}, /*index=5*/bf16[96,1024]{1,0:T(8,128)(2,1)S(1)}) custom-call(f32[16,3,4,128]{3,2,1,0:T(4,128)S(1)} %all_to_all.101.refs_0_.recv_ref, ...), custom_call_target="tpu_custom_call" | custom-call | flops 40000000 | bytes 1000 | tf_op jit(solution)/shard_map/pallas_call | solution.py:455
  147.1 0.5 slice.9
  148.1 6.7 %all-to-all-done.13.recv_ref = f32[32,2,4,128]{3,2,1,0:T(4,128)S(1)} async-done(((f32[32,2,4,128]{3,2,1,0:T(4,128)}), f32[32,2,4,128]{3,2,1,0:T(4,128)S(1)}, u32[]{:S(2)}, u32[]{:S(2)}) %all-to-all-start.13) | async-done | bytes 131104 | tf_op jit(solution)/shard_map/all_to_all | solution.py:467
  154.8 2.3 %shard_map.41 = f32[512,1024]{1,0:T(8,128)} custom-call(f32[512,1024]{1,0:T(8,128)S(1)} %get-tuple-element.346.a_ref.refs_0_, f32[32,2,4,128]{3,2,1,0:T(4,128)S(1)} %all-to-all-done.13.recv_ref, f32[128,128]{1,0:T(8,128)S(1)} %get-tuple-element.380.q_ref, f32[128,128]{1,0:T(8,128)S(1)} %get-tuple-element.381.side_ref, ...), custom_call_target="tpu_custom_call" | custom-call | tf_op jit(solution)/shard_map/pallas_call | solution.py:527
  157.2 0.2 while.39
Async XLA Ops:
  141.1 13.7 %all-to-all-start.13 = ((f32[32,2,4,128]{3,2,1,0:T(4,128)}), f32[32,2,4,128]{3,2,1,0:T(4,128)S(1)}, u32[]{:S(2)}, u32[]{:S(2)}) async-start(f32[32,2,4,128]{3,2,1,0:T(4,128)} %shard_map.40), calls=%async_computation.13 | async-start | bytes 262144 | tf_op jit(solution)/shard_map/all_to_all | solution.py:467

commit v8 on v7

--- a/solution.py
+++ b/solution.py
@@ -61,32 +61,28 @@
     return jnp.concatenate(out, axis=0)
 
 
-def send_all(send_ref, first, parts):
+def send_all(send_ref, first, x):
+    height = send_ref.shape[2]
     for member in range(send_ref.shape[0]):
-        for k, part in enumerate(parts):
-            send_ref[member, first + k] = part
-
-
-def halves(x):
-    return [x[:4], x[4:]]
-
-
-def along_cols(recv_ref):
-    s = jnp.sum(recv_ref[:, 0:2], axis=0)
-    return jnp.concatenate([s[0], s[1]], axis=0)
-
-
-def along_rows(recv_ref):
-    return jnp.sum(recv_ref[:, 0], axis=0)
-
-
-def whole_from_rows(recv_ref, group):
-    return jnp.concatenate([recv_ref[r, group] for r in range(recv_ref.shape[0])], axis=0)
-
-
-def whole_from_cols(recv_ref, group):
+        for k in range(x.shape[0] // height):
+            send_ref[member, first // height + k] = x[k * height : (k + 1) * height]
+
+
+def taken(recv_ref, member, first, count):
+    height = recv_ref.shape[2]
+    return [recv_ref[member, first // height + k] for k in range(count // height)]
+
+
+def summed(recv_ref, count):
+    height = recv_ref.shape[2]
+    blocks = [jnp.sum(recv_ref[:, k], axis=0) for k in range(count // height)]
+    return jnp.concatenate(blocks, axis=0)
+
+
+def gathered(recv_ref, first, count):
+    members = range(recv_ref.shape[0])
     return jnp.concatenate(
-        [recv_ref[c, group + k] for c in range(recv_ref.shape[0]) for k in range(2)], axis=0
+        [block for m in members for block in taken(recv_ref, m, first, count)], axis=0
     )
 
 
@@ -118,8 +114,8 @@
     column = recv_ref[0, 0]
     piece_ref[...] = recv_ref[0, 1]
     packed = recv_ref[0, 1][2:3]
-    send_all(send_ref, 0, halves(times_rows(a_ref, without_first(column, ids_ref[0]))))
-    send_all(send_ref, 2, [column])
+    send_all(send_ref, 0, times_rows(a_ref, without_first(column, ids_ref[0])))
+    send_all(send_ref, 8, column)
     blank = jnp.zeros((1, LANES), F32)
     for member in range(32):
         j, quarter = member // 4, member % 4
@@ -166,16 +162,17 @@
 
 def given_rows(recv_ref, by_rows):
     row_index, col_index = places()
+    height = recv_ref.shape[2]
     if by_rows:
-        group = 2 if recv_ref.shape[1] > 2 else 0
-        here = recv_ref[row_index, group]
-        there = [recv_ref[2 * col_index + k, group] for k in range(2)]
-        first = recv_ref[0, group][0:1]
+        start = 8 if recv_ref.shape[1] * height > 8 else 0
+        here = taken(recv_ref, row_index, start, 4)
+        there = taken(recv_ref, 2 * col_index, start, 4) + taken(recv_ref, 2 * col_index + 1, start, 4)
     else:
-        here = recv_ref[row_index // 2, 1 + row_index % 2]
-        there = [recv_ref[col_index, 1 + k] for k in range(2)]
-        first = recv_ref[0, 1][0:1]
-    return jnp.concatenate([here, *there, first, jnp.zeros((3, LANES), F32)], axis=0)
+        start, half = 4, row_index % 2 * (4 // height)
+        here = [recv_ref[row_index // 2, half + (start // height + k)] for k in range(4 // height)]
+        there = taken(recv_ref, col_index, start, 8)
+    first = recv_ref[0, start // height][0:1]
+    return jnp.concatenate([*here, *there, first, jnp.zeros((3, LANES), F32)], axis=0)
 
 
 def kept_rows(ref):
@@ -214,10 +211,10 @@
 
     even = step % 2 == 0
     if even:
-        y_here, given = along_cols(recv_ref), whole_from_rows(recv_ref, 2)
+        y_here, given = summed(recv_ref, 8), gathered(recv_ref, 8, 4)
         chunk, count, part = col_index, 8, slice(4, 12)
     else:
-        y_here, given = along_rows(recv_ref), whole_from_cols(recv_ref, 1)
+        y_here, given = summed(recv_ref, 4), gathered(recv_ref, 4, 8)
         chunk, count, part = row_index, 4, slice(0, 4)
     if step > 2:
         rows_refs[step - 2][...] = product_rows(step, recv_ref, scal, q_refs)
@@ -238,21 +235,21 @@
         here = here - length * q_refs[step - 2][at, :]
     here = without_first(here, chunk)
     if even:
-        send_all(send_ref, 0, [times_cols(a_ref, here)])
-        send_all(send_ref, 1, halves(here))
+        send_all(send_ref, 0, times_cols(a_ref, here))
+        send_all(send_ref, 4, here)
     else:
-        send_all(send_ref, 0, halves(times_rows(a_ref, here)))
-        send_all(send_ref, 2, [here])
+        send_all(send_ref, 0, times_rows(a_ref, here))
+        send_all(send_ref, 8, here)
     if step == 2:
-        send_all(send_ref, 3, [piece_ref[...]])
-    if step == 2:
+        send_all(send_ref, 12, piece_ref[0:2, :])
         new_piece_ref[...] = recv_ref[0, 3]
     if step == 3:
-        edge_ref[...] = jnp.concatenate([recv_ref[c, 3][0:2] for c in range(16)], axis=0)
+        edge_ref[...] = gathered(recv_ref, 12, 2)
 
 
 def last_send_kernel(recv_ref, piece_ref, send_ref):
-    send_all(send_ref, 0, [along_rows(recv_ref), piece_ref[...]])
+    send_all(send_ref, 0, summed(recv_ref, 4))
+    send_all(send_ref, 4, piece_ref[0:2, :])
 
 
 def sign(k):
@@ -299,7 +296,7 @@
     aq_rows = {i: refs[17 + i] for i in range(1, 7)}
     q_out, flag_ref, reflect_ref, side_ref, left_ref, right_ref, rows_out = refs[24:31]
     q, length, _, _, cs, scal = settle(
-        9, whole_from_cols(recv_ref, 1), scal_refs[7][...], {i: r[...] for i, r in q_refs.items()}
+        9, gathered(recv_ref, 4, 8), scal_refs[7][...], {i: r[...] for i, r in q_refs.items()}
     )
     q_out[...] = q
     rows_out[...] = product_rows(9, recv_ref, scal_refs[7][...], q_refs)
@@ -397,17 +394,17 @@
     for t in range(8):
         members = [divmod(8 * k + t, 2) for k in range(8)]
         high, middle, low = three(
-            jnp.concatenate([recv_ref[r, 1][i : i + 1] for r, i in members], axis=0)
+            jnp.concatenate([recv_ref[r, 2][i : i + 1] for r, i in members], axis=0)
         )
         stack = jnp.concatenate([high, middle, high, middle, low, high], axis=0)
         edge_ref[:, t * LANES : (t + 1) * LANES] = stack.astype(jnp.bfloat16)
     inverse = coefficient(side_ref, 96)
     aq = (given_rows(recv_ref, True) - side_ref[104:120, :]) * inverse
-    alpha = total(q_ref[...] * whole_from_rows(recv_ref, 0)) - coefficient(side_ref, 120)
+    alpha = total(q_ref[...] * gathered(recv_ref, 0, 4)) - coefficient(side_ref, 120)
     alpha = alpha * inverse
     lanes = iota((1, LANES), 1)
     shifted = pltpu.roll(aq[12:13, :], LANES - 1, 1)
-    added = jnp.where(lanes == 7, 0.5 * alpha, 0.0) - jnp.where(lanes < 8, shifted, 0.0)
+    added = -jnp.where(lanes < 8, shifted, 0.0)
     added = jnp.concatenate([added, jnp.zeros((7, LANES), F32)], axis=0).T[0:8, 0:1]
 
     def last(count, first, kept):
@@ -422,7 +419,8 @@
     blank = jnp.zeros((6, LANES), F32)
     copies = []
     for q in range(4):
-        upright = jnp.concatenate([side_ref[8 * q + 7 : 8 * q + 8, :], ws_r[q], blank], axis=0).T
+        slope = side_ref[8 * q + 7 : 8 * q + 8, :]
+        upright = jnp.concatenate([slope, ws_r[q] - alpha * slope, blank], axis=0).T
         for half in range(2):
             at = slice(q * LANES + half * 64, q * LANES + half * 64 + 64)
             piece = upright[half * 64 : half * 64 + 64]
@@ -488,8 +486,8 @@
         if step > 2:
             args.append(scals[step - 2])
         args += [qs[i] for i in range(1, step - 1)] + [aq_rows[i] for i in range(1, step - 2)]
-        groups = 4 if step == 2 else 3
-        outs = [(16 if step % 2 == 0 else 32, groups, 4, LANES), whole]
+        message = (7, 2, LANES) if step == 2 else (3, 4, LANES)
+        outs = [(16 if step % 2 == 0 else 32, *message), whole]
         if step > 2:
             outs.append((16, LANES))
         outs.append((16, LANES))
@@ -508,7 +506,7 @@
         if step == 2:
             piece = packed = result.pop(0)
         recv = exchange(send, "col" if step % 2 == 0 else "row")
-    (send,) = call(last_send_kernel, [(32, 2, 4, LANES)], recv, packed)
+    (send,) = call(last_send_kernel, [(32, 3, 2, LANES)], recv, packed)
     last = exchange(send, "row")
     rows, cols = matrix.shape
     q, flag, reflect, side, left, right = call(

time: 158 us -> 157 us (level)
  no operation moved by 1% of the time
where the time goes in v8:
time: 157 us
  blocking collectives  134 us (85%)
  Pallas kernels  9.97 us (6%)
  waiting for transfers between devices  6.37 us (4%)
  starting transfers between devices  3.86 us (2%)
    all_to_all x9, blocking collectives, exchange(): return lax.all_to_all(x, axis, 0, 0, tiled=True)  134 us
    all_to_all x1, waiting for transfers between devices, exchange(): return lax.all_to_all(x, axis, 0, 0, tiled=True)  6.37 us
    pallas_call x10, Pallas kernels, call(): pl.pallas_call(kernel, out_shape=[shape(x) for x in outs], in_specs=[pl.B...  5.98 us
    all_to_all x1, starting transfers between devices, exchange(): return lax.all_to_all(x, axis, 0, 0, tiled=True)  3.86 us
  transfers between devices with their start and end apart: 1, of which 1 were waited for; matrix products, arithmetic and copies ran while one was open for 0% of the time, Pallas kernels for 1%

profile of v8, /device:TPU:1, one launch (start us, length us, event | category | flops | bytes accessed | tf_op | source)
XLA Modules:
  0.0 156.8 jit_solution(2494982943578230685)
XLA Ops:
  0.6 1.7 %shard_map.30 = (f32[16,2,4,128]{3,2,1,0:T(4,128)S(1)}, f32[512,1024]{1,0:T(8,128)S(1)}) custom-call(f32[512,1024]{1,0:T(8,128)} %a_ref.1), custom_call_target="tpu_custom_call" | custom-call | tf_op jit(solution)/shard_map/pallas_call | solution.py:470
  2.4 17.1 %all_to_all.93.recv_ref = f32[16,2,4,128]{3,2,1,0:T(4,128)S(1)} all-to-all(f32[16,2,4,128]{3,2,1,0:T(4,128)S(1)} %get-tuple-element.347), channel_id=1, replica_groups=mesh['row'=32,'col'=16] {'col'}, dimensions={0} | all-to-all | bytes 131072 | tf_op jit(solution)/shard_map/all_to_all | solution.py:465
  19.4 0.3 shard_map.31
  19.7 23.6 %all_to_all.94.refs_1_ = f32[32,4,4,128]{3,2,1,0:T(4,128)S(1)} all-to-all(f32[32,4,4,128]{3,2,1,0:T(4,128)S(1)} %get-tuple-element.348), channel_id=1, replica_groups=mesh['row'=32,'col'=16] {'row'}, dimensions={0} | all-to-all | bytes 524288 | tf_op jit(solution)/shard_map/all_to_all | solution.py:465
  43.3 0.3 shard_map.32
  43.7 13.4 %all_to_all.95.refs_1_ = f32[16,7,2,128]{3,2,1,0:T(2,128)S(1)} all-to-all(f32[16,7,2,128]{3,2,1,0:T(2,128)S(1)} %get-tuple-element.350), channel_id=1, replica_groups=mesh['row'=32,'col'=16] {'col'}, dimensions={0} | all-to-all | bytes 229376 | tf_op jit(solution)/shard_map/all_to_all | solution.py:465
  57.1 0.5 shard_map.33
  57.6 14.2 %all_to_all.96.refs_1_ = f32[32,3,4,128]{3,2,1,0:T(4,128)S(1)} all-to-all(f32[32,3,4,128]{3,2,1,0:T(4,128)S(1)} %get-tuple-element.353), channel_id=1, replica_groups=mesh['row'=32,'col'=16] {'row'}, dimensions={0} | all-to-all | bytes 393216 | tf_op jit(solution)/shard_map/all_to_all | solution.py:465
  71.8 0.4 shard_map.34
  72.2 12.7 %all_to_all.97.refs_1_ = f32[16,3,4,128]{3,2,1,0:T(4,128)S(1)} all-to-all(f32[16,3,4,128]{3,2,1,0:T(4,128)S(1)} %get-tuple-element.357), channel_id=1, replica_groups=mesh['row'=32,'col'=16] {'col'}, dimensions={0} | all-to-all | bytes 196608 | tf_op jit(solution)/shard_map/all_to_all | solution.py:465
  84.8 0.5 shard_map.35
  85.3 13.8 %all_to_all.98.refs_1_ = f32[32,3,4,128]{3,2,1,0:T(4,128)S(1)} all-to-all(f32[32,3,4,128]{3,2,1,0:T(4,128)S(1)} %get-tuple-element.361), channel_id=1, replica_groups=mesh['row'=32,'col'=16] {'row'}, dimensions={0} | all-to-all | bytes 393216 | tf_op jit(solution)/shard_map/all_to_all | solution.py:465
  99.1 0.4 shard_map.36
  99.5 12.9 %all_to_all.99.refs_1_ = f32[16,3,4,128]{3,2,1,0:T(4,128)S(1)} all-to-all(f32[16,3,4,128]{3,2,1,0:T(4,128)S(1)} %get-tuple-element.365), channel_id=1, replica_groups=mesh['row'=32,'col'=16] {'col'}, dimensions={0} | all-to-all | bytes 196608 | tf_op jit(solution)/shard_map/all_to_all | solution.py:465
  112.4 0.5 shard_map.37
  112.9 13.8 %all_to_all.100.refs_1_ = f32[32,3,4,128]{3,2,1,0:T(4,128)S(1)} all-to-all(f32[32,3,4,128]{3,2,1,0:T(4,128)S(1)} %get-tuple-element.369), channel_id=1, replica_groups=mesh['row'=32,'col'=16] {'row'}, dimensions={0} | all-to-all | bytes 393216 | tf_op jit(solution)/shard_map/all_to_all | solution.py:465
  126.8 0.4 shard_map.38
  127.2 12.9 %all_to_all.101.refs_0_.recv_ref = f32[16,3,4,128]{3,2,1,0:T(4,128)S(1)} all-to-all(f32[16,3,4,128]{3,2,1,0:T(4,128)S(1)} %get-tuple-element.373), channel_id=1, replica_groups=mesh['row'=32,'col'=16] {'col'}, dimensions={0} | all-to-all | bytes 196608 | tf_op jit(solution)/shard_map/all_to_all | solution.py:465
  140.1 0.7 shard_map.40
  140.8 3.9 %all-to-all-start.13 = ((f32[32,3,2,128]{3,2,1,0:T(2,128)}), f32[32,3,2,128]{3,2,1,0:T(2,128)S(1)}, u32[]{:S(2)}, u32[]{:S(2)}) async-start(f32[32,3,2,128]{3,2,1,0:T(2,128)} %shard_map.40), calls=%async_computation.13 | async-start | bytes 196608 | tf_op jit(solution)/shard_map/all_to_all | solution.py:465
  144.6 2.1 %shard_map.39 = (f32[128,128]{1,0:T(8,128)S(1)}, f32[8,128]{1,0:T(8,128)S(1)}, f32[8,512]{1,0:T(8,128)}, f32[128,128]{1,0:T(8,128)S(1)}, bf16[512,256]{1,0:T(8,128)(2,1)S(1)}, /*index=5*/bf16[96,1024]{1,0:T(8,128)(2,1)S(1)}) custom-call(f32[16,3,4,128]{3,2,1,0:T(4,128)S(1)} %all_to_all.101.refs_0_.recv_ref, ...), custom_call_target="tpu_custom_call" | custom-call | flops 40000000 | bytes 1000 | tf_op jit(solution)/shard_map/pallas_call | solution.py:453
  146.7 0.5 slice.9
  147.8 6.4 %all-to-all-done.13.recv_ref = f32[32,3,2,128]{3,2,1,0:T(2,128)S(1)} async-done(((f32[32,3,2,128]{3,2,1,0:T(2,128)}), f32[32,3,2,128]{3,2,1,0:T(2,128)S(1)}, u32[]{:S(2)}, u32[]{:S(2)}) %all-to-all-start.13) | async-done | bytes 98336 | tf_op jit(solution)/shard_map/all_to_all | solution.py:465
  154.2 2.3 %shard_map.41 = f32[512,1024]{1,0:T(8,128)} custom-call(f32[512,1024]{1,0:T(8,128)S(1)} %get-tuple-element.346.a_ref.refs_0_, f32[32,3,2,128]{3,2,1,0:T(2,128)S(1)} %all-to-all-done.13.recv_ref, f32[128,128]{1,0:T(8,128)S(1)} %get-tuple-element.380.q_ref, f32[128,128]{1,0:T(8,128)S(1)} %get-tuple-element.381.side_ref, ...), custom_call_target="tpu_custom_call" | custom-call | tf_op jit(solution)/shard_map/pallas_call | solution.py:525
  156.5 0.2 while.39
Async XLA Ops:
  140.8 13.4 %all-to-all-start.13 = ((f32[32,3,2,128]{3,2,1,0:T(2,128)}), f32[32,3,2,128]{3,2,1,0:T(2,128)S(1)}, u32[]{:S(2)}, u32[]{:S(2)}) async-start(f32[32,3,2,128]{3,2,1,0:T(2,128)} %shard_map.40), calls=%async_computation.13 | async-start | bytes 196608 | tf_op jit(solution)/shard_map/all_to_all | solution.py:465
